TPU v7x, 128 devices: a whole 4x4x4 slice. The times are simulated.
128 devices in a mesh: grp: 8 (over z, core), dev: 16 (over x, y).
Axes of the slice: x: 4, y: 4, z: 4, core: 2. Of those that a mesh axis runs over, the one named last changes fastest.
Arguments:
- candidates: bfloat16 [262144, 512], P(('grp', 'dev')), may hold values from -6 to 6
- prefix_keys: bfloat16 [128, 1024, 512], P(('grp', 'dev')), may hold values from -6 to 6
- prefix_values: bfloat16 [128, 1024, 512], P(('grp', 'dev')), may hold values from -6 to 6
- cand_count: int32 [128], P(('grp', 'dev')), may hold values from 128 to 2048, as said below
- prefix_len: int32 [128], P(('grp', 'dev')), may hold values from 128 to 1024, as said below
- dest_device: int32 [2048], P(('grp', 'dev')), may hold values from 0 to 127, as said below
- dest_slot: int32 [2048], P(('grp', 'dev')), may hold values from 0 to 15, as said below
- norm_gain: float32 [512], replicated, may hold values from 0.5 to 1.5
- w_in: bfloat16 [512, 2048], replicated, may hold values from -0.25 to 0.25
- b_in: float32 [2048], replicated, may hold values from -3 to 3
- attn_gain: float32 [512], replicated, may hold values from 0.5 to 1.5
- w_out: bfloat16 [512, 512], replicated, may hold values from -0.25 to 0.25
Outputs:
- owned_blocks: bfloat16 [262144, 512], P(('grp', 'dev'))
Inputs may be any that keep to these rules, and one draw needn't show every extreme that they name: `cand_count`: some user reaches the largest count in every draw. `prefix_len`: some user reaches the largest length in every draw. `dest_device`: devices are numbered in the order grp then dev. The 16 blocks of one device go to distinct devices, 2 of them to each index of grp and 1 to each index of dev. For every index of dev, the blocks that the devices with that index send to one index of grp go 1 to each index of dev. For every index of grp, the blocks that the devices with that index send to one index of dev go 2 to each index of grp. Every device receives exactly 16 blocks. `dest_slot`: the blocks that one device receives fill its 16 block offsets once each.
All inputs are finite; a program needn't handle non-finite values.
Results may differ from a plain program's by a relative error of at most 0.0057.
Values may be sent and summed in bfloat16 or wider, within the bound.
A program may use at most 128 MiB of HBM per device.

v0:
```python
import jax
import jax.numpy as jnp
from jax import lax
from jax.sharding import PartitionSpec as P

HEADS = 4
BLK = 128


def normalize(matrix, gain):
    average = jnp.mean(matrix, axis=-1, keepdims=True)
    centred = matrix - average
    spread = jnp.mean(centred * centred, axis=-1, keepdims=True)
    return centred * lax.rsqrt(spread + 1e-06) * gain


def user_output(
    cand_rows, key_rows, value_rows, live_count, length, norm_gain, w_in, b_in, attn_gain, w_out
):
    row_total = cand_rows.shape[0]
    model_width = cand_rows.shape[1]
    head_dim = model_width // HEADS
    scale = 1.0 / jnp.sqrt(jnp.float32(head_dim))
    block_rows = min(512, row_total)
    prefix_k = key_rows.reshape(-1, HEADS, head_dim)
    prefix_v = value_rows.reshape(-1, HEADS, head_dim)
    key_live = jnp.arange(prefix_k.shape[0], dtype=jnp.int32) < length

    def one_block(block_index):
        first_row = block_index * block_rows
        block_in = lax.dynamic_slice_in_dim(cand_rows, first_row, block_rows, 0)
        inputs_f = block_in.astype(jnp.float32)
        normed = normalize(inputs_f, norm_gain).astype(jnp.bfloat16)
        projected = jax.nn.silu(
            jnp.dot(normed, w_in, preferred_element_type=jnp.float32) + b_in
        ).astype(jnp.bfloat16)
        gate_part, value_part, query_part, key_part = jnp.split(projected, 4, axis=1)
        queries = query_part.reshape(block_rows, HEADS, head_dim)
        own_keys = key_part.reshape(block_rows, HEADS, head_dim)
        own_values = value_part.reshape(block_rows, HEADS, head_dim)
        scores = (
            jnp.einsum("rhd,jhd->hrj", queries, prefix_k, preferred_element_type=jnp.float32)
            * scale
        )
        weights = jnp.where(key_live[None, None, :], jax.nn.silu(scores), 0.0).astype(jnp.bfloat16)
        self_score = (
            jnp.sum(queries.astype(jnp.float32) * own_keys.astype(jnp.float32), axis=-1) * scale
        )
        self_weight = jax.nn.silu(self_score).astype(jnp.bfloat16)
        attended = jnp.einsum("hrj,jhd->rhd", weights, prefix_v, preferred_element_type=jnp.float32)
        attended = attended + self_weight.astype(jnp.float32)[:, :, None] * own_values.astype(
            jnp.float32
        )
        attended = attended.reshape(block_rows, model_width)
        gated_rows = (normalize(attended, attn_gain) * gate_part.astype(jnp.float32)).astype(
            jnp.bfloat16
        )
        layer_out = inputs_f + jnp.dot(gated_rows, w_out, preferred_element_type=jnp.float32)
        live_rows = first_row + jnp.arange(block_rows, dtype=jnp.int32) < live_count
        return jnp.where(live_rows[:, None], layer_out, 0.0).astype(jnp.bfloat16)

    outputs = lax.map(one_block, jnp.arange(row_total // block_rows, dtype=jnp.int32))
    return outputs.reshape(row_total, model_width)


def positions(groups, group_total, per_group):
    matches = (groups[:, None] == jnp.arange(group_total, dtype=jnp.int32)[None, :]).astype(
        jnp.int32
    )
    rank_in = jnp.sum((jnp.cumsum(matches, axis=0) - matches) * matches, axis=1)
    placed = groups * per_group + rank_in
    return jnp.zeros_like(groups).at[placed].set(jnp.arange(groups.shape[0], dtype=jnp.int32))


def shards(
    candidates,
    prefix_keys,
    prefix_values,
    cand_count,
    prefix_len,
    dest_device,
    dest_slot,
    norm_gain,
    w_in,
    b_in,
    attn_gain,
    w_out,
):
    model_width = candidates.shape[1]
    scored = user_output(
        candidates,
        prefix_keys[0],
        prefix_values[0],
        cand_count[0],
        prefix_len[0],
        norm_gain,
        w_in,
        b_in,
        attn_gain,
        w_out,
    )
    blocks = scored.reshape(-1, BLK, model_width)
    block_total = blocks.shape[0]
    group_count = lax.axis_size("grp")
    member_count = lax.axis_size("dev")
    target_group = dest_device // member_count
    target_member = dest_device % member_count
    per_group = block_total // group_count
    per_member = block_total // member_count
    first_order = positions(target_group, group_count, per_group)
    outgoing = blocks[first_order].reshape(group_count, per_group, BLK, model_width)
    meta_out = jnp.stack([target_member, dest_slot], axis=1)[first_order].reshape(
        group_count, per_group, 2
    )
    received, meta_in = (
        lax.all_to_all(outgoing, "grp", split_axis=0, concat_axis=0, tiled=True),
        lax.all_to_all(meta_out, "grp", split_axis=0, concat_axis=0, tiled=True),
    )
    received = received.reshape(block_total, BLK, model_width)
    meta_in = meta_in.reshape(block_total, 2)
    second_order = positions(meta_in[:, 0], member_count, per_member)
    onward = received[second_order].reshape(member_count, per_member, BLK, model_width)
    slot_onward = meta_in[second_order, 1].reshape(member_count, per_member)
    landed, slot_in = (
        lax.all_to_all(onward, "dev", split_axis=0, concat_axis=0, tiled=True),
        lax.all_to_all(slot_onward, "dev", split_axis=0, concat_axis=0, tiled=True),
    )
    landed = landed.reshape(block_total, BLK, model_width)
    slot_in = slot_in.reshape(block_total)
    source_of = (
        jnp.zeros((block_total,), jnp.int32)
        .at[slot_in]
        .set(jnp.arange(block_total, dtype=jnp.int32))
    )
    arrived = landed[source_of]
    return arrived.reshape(block_total * BLK, model_width)


def solution(mesh):
    return jax.shard_map(
        shards,
        mesh=mesh,
        in_specs=(
            P(("grp", "dev"), None),
            P(("grp", "dev"), None, None),
            P(("grp", "dev"), None, None),
            P(("grp", "dev")),
            P(("grp", "dev")),
            P(("grp", "dev")),
            P(("grp", "dev")),
            P(),
            P(),
            P(),
            P(),
            P(),
        ),
        out_specs=P(("grp", "dev"), None),
        check_vma=False,
    )
```

profile of v0, /device:TPU:0, one launch (start us, length us, event | category | flops | bytes accessed | tf_op | source)
XLA Modules:
  0.0 182.7 jit_solution(12087476206181074044)
XLA Ops:
  0.0 0.7 fusion.37
  1.0 0.6 scatter_custom_fusion
  1.6 0.7 pad_add_fusion
  2.9 0.7 copy.62
  3.7 5.4 %all-to-all-start.1 = ((s32[8,2,2]{1,2,0:T(2,128)}), s32[8,2,2]{1,2,0:T(2,128)S(1)}, u32[]{:S(2)}, u32[]{:S(2)}) async-start(s32[8,2,2]{1,2,0:T(2,128)} %copy.62), calls=%async_computation.1 | async-start | bytes 16384 | tf_op jit(solution)/shard_map/all_to_all | solution.py:117
  9.1 1.6 copy.57
  10.7 1.3 copy.59
  12.0 1.3 copy.58
  13.4 85.1 %while.11 = (s32[]{:T(128)}, bf16[4,512,512]{2,1,0:T(8,128)(2,1)}, s32[4]{0:T(128)S(1)}, s32[]{:T(128)}, bf16[2048,512]{1,0:T(8,128)(2,1)}, /*index=5*/f32[512]{...) while((s32[]{:T(128)}, bf16[4,512,512]{2,1,0:T(8,128)(2,1)}, ...), condition=%wide.region_6.7_spmd.clone, body=%wide.region_0.6_spmd.clone.sunk | while | flops 2445294592 | bytes 43093328 | solution.py:62
  13.4 0.7 dynamic_slice.25
  14.8 1.2 convert_reduce_fusion.2
  16.0 1.3 fusion.71
  17.3 3.5 %multiply_convert_fusion.6 = bf16[512,2048]{1,0:T(8,128)(2,1)S(1)} fusion(bf16[512,2048]{1,0:T(8,128)(2,1)} %get-tuple-element.321, f32[2048]{0:T(1024)S(1)} %get-tuple-element.322, f32[512]{0:T(512)S(1)} %get-tuple-element.320, f32[512]{0:T(512)S(1)} %add_rsqrt_fusion.4, f32[512]{0:T(512)S(1)} %broadcast_multiply_fusion.4, ...), kind=kOutput, calls=%fused_computation.10.clone.1 | convolution fusion | flops 1081344000 | bytes 4732932 | tf_op jit(solution)/shard_map/while/body/eval_jaxpr/dot_general | solution.py:35
  21.2 1.0 copy-done
  22.2 1.3 copy.82
  24.0 0.6 multiply_reduce_fusion.4
  24.8 0.7 iota_compare_fusion.4
  25.5 5.5 %fusion.74 = (f32[512]{0:T(512)S(1)}, f32[512,4,128]{0,2,1:T(8,128)S(1)}) fusion(f32[512,4,128]{0,2,1:T(8,128)S(1)} %bitcast.71, f32[512,4]{0,1:T(4,128)S(1)} %fusion.73, bf16[1024,4,128]{0,2,1:T(8,128)(2,1)} %get-tuple-element.324, pred[1024]{0:T(1024)(128)(4,1)S(1)} %iota_compare_fusion.4, bf16[1024,4,128]{2,0,1:T(8,128)(2,1)} %get-tuple-element.323, ...), kind=kOutput, calls=%fused_computation.90.clone.1 | convolution fusion | flops 1089207808 | bytes 4729856 | tf_op jit(solution)/shard_map/while/body/eval_jaxpr/hrj,jhd->rhd/dot_general | solution.py:50
  31.5 0.7 add_compare_fusion.2
  32.2 2.5 %fusion.75 = bf16[4,512,512]{2,1,0:T(8,128)(2,1)} fusion(bf16[4,512,512]{2,1,0:T(8,128)(2,1)} %get-tuple-element.299, s32[]{:T(128)S(6)} %copy.88, bf16[512,512]{1,0:T(8,128)(2,1)S(1)} %copy-done.3, f32[512,512]{1,0:T(8,128)S(1)} %copy.84, bf16[512,2048]{1,0:T(8,128)(2,1)} %copy-done, f32[512]{0:T(512)S(1)} %get-tuple-element.325, ...), kind=kOutput, calls=%fused_computation.23.clone.1 | convolution fusion | flops 271056896 | bytes 3152392 | tf_op jit(solution)/shard_map/while/body/eval_jaxpr/dot_general | solution.py:58
  34.7 0.7 dynamic_slice.25
  36.0 1.2 convert_reduce_fusion.2
  37.2 1.3 fusion.71
  38.6 3.5 %multiply_convert_fusion.6 = bf16[512,2048]{1,0:T(8,128)(2,1)S(1)} fusion(bf16[512,2048]{1,0:T(8,128)(2,1)} %get-tuple-element.321, f32[2048]{0:T(1024)S(1)} %get-tuple-element.322, f32[512]{0:T(512)S(1)} %get-tuple-element.320, f32[512]{0:T(512)S(1)} %add_rsqrt_fusion.4, f32[512]{0:T(512)S(1)} %broadcast_multiply_fusion.4, ...), kind=kOutput, calls=%fused_computation.10.clone.1 | convolution fusion | flops 1081344000 | bytes 4732932 | tf_op jit(solution)/shard_map/while/body/eval_jaxpr/dot_general | solution.py:35
  42.5 1.0 copy-done
  43.5 1.3 copy.82
  45.3 0.6 multiply_reduce_fusion.4
  46.1 0.7 iota_compare_fusion.4
  46.7 5.5 %fusion.74 = (f32[512]{0:T(512)S(1)}, f32[512,4,128]{0,2,1:T(8,128)S(1)}) fusion(f32[512,4,128]{0,2,1:T(8,128)S(1)} %bitcast.71, f32[512,4]{0,1:T(4,128)S(1)} %fusion.73, bf16[1024,4,128]{0,2,1:T(8,128)(2,1)} %get-tuple-element.324, pred[1024]{0:T(1024)(128)(4,1)S(1)} %iota_compare_fusion.4, bf16[1024,4,128]{2,0,1:T(8,128)(2,1)} %get-tuple-element.323, ...), kind=kOutput, calls=%fused_computation.90.clone.1 | convolution fusion | flops 1089207808 | bytes 4729856 | tf_op jit(solution)/shard_map/while/body/eval_jaxpr/hrj,jhd->rhd/dot_general | solution.py:50
  52.8 0.7 add_compare_fusion.2
  53.4 2.5 %fusion.75 = bf16[4,512,512]{2,1,0:T(8,128)(2,1)} fusion(bf16[4,512,512]{2,1,0:T(8,128)(2,1)} %get-tuple-element.299, s32[]{:T(128)S(6)} %copy.88, bf16[512,512]{1,0:T(8,128)(2,1)S(1)} %copy-done.3, f32[512,512]{1,0:T(8,128)S(1)} %copy.84, bf16[512,2048]{1,0:T(8,128)(2,1)} %copy-done, f32[512]{0:T(512)S(1)} %get-tuple-element.325, ...), kind=kOutput, calls=%fused_computation.23.clone.1 | convolution fusion | flops 271056896 | bytes 3152392 | tf_op jit(solution)/shard_map/while/body/eval_jaxpr/dot_general | solution.py:58
  55.9 0.7 dynamic_slice.25
  57.3 1.2 convert_reduce_fusion.2
  58.5 1.3 fusion.71
  59.9 3.5 %multiply_convert_fusion.6 = bf16[512,2048]{1,0:T(8,128)(2,1)S(1)} fusion(bf16[512,2048]{1,0:T(8,128)(2,1)} %get-tuple-element.321, f32[2048]{0:T(1024)S(1)} %get-tuple-element.322, f32[512]{0:T(512)S(1)} %get-tuple-element.320, f32[512]{0:T(512)S(1)} %add_rsqrt_fusion.4, f32[512]{0:T(512)S(1)} %broadcast_multiply_fusion.4, ...), kind=kOutput, calls=%fused_computation.10.clone.1 | convolution fusion | flops 1081344000 | bytes 4732932 | tf_op jit(solution)/shard_map/while/body/eval_jaxpr/dot_general | solution.py:35
  63.8 1.0 copy-done
  64.8 1.3 copy.82
  67.3 0.7 iota_compare_fusion.4
  68.0 5.5 %fusion.74 = (f32[512]{0:T(512)S(1)}, f32[512,4,128]{0,2,1:T(8,128)S(1)}) fusion(f32[512,4,128]{0,2,1:T(8,128)S(1)} %bitcast.71, f32[512,4]{0,1:T(4,128)S(1)} %fusion.73, bf16[1024,4,128]{0,2,1:T(8,128)(2,1)} %get-tuple-element.324, pred[1024]{0:T(1024)(128)(4,1)S(1)} %iota_compare_fusion.4, bf16[1024,4,128]{2,0,1:T(8,128)(2,1)} %get-tuple-element.323, ...), kind=kOutput, calls=%fused_computation.90.clone.1 | convolution fusion | flops 1089207808 | bytes 4729856 | tf_op jit(solution)/shard_map/while/body/eval_jaxpr/hrj,jhd->rhd/dot_general | solution.py:50
  74.0 0.7 add_compare_fusion.2
  74.7 2.5 %fusion.75 = bf16[4,512,512]{2,1,0:T(8,128)(2,1)} fusion(bf16[4,512,512]{2,1,0:T(8,128)(2,1)} %get-tuple-element.299, s32[]{:T(128)S(6)} %copy.88, bf16[512,512]{1,0:T(8,128)(2,1)S(1)} %copy-done.3, f32[512,512]{1,0:T(8,128)S(1)} %copy.84, bf16[512,2048]{1,0:T(8,128)(2,1)} %copy-done, f32[512]{0:T(512)S(1)} %get-tuple-element.325, ...), kind=kOutput, calls=%fused_computation.23.clone.1 | convolution fusion | flops 271056896 | bytes 3152392 | tf_op jit(solution)/shard_map/while/body/eval_jaxpr/dot_general | solution.py:58
  77.2 0.7 dynamic_slice.25
  78.6 1.2 convert_reduce_fusion.2
  79.8 1.3 fusion.71
  81.1 3.5 %multiply_convert_fusion.6 = bf16[512,2048]{1,0:T(8,128)(2,1)S(1)} fusion(bf16[512,2048]{1,0:T(8,128)(2,1)} %get-tuple-element.321, f32[2048]{0:T(1024)S(1)} %get-tuple-element.322, f32[512]{0:T(512)S(1)} %get-tuple-element.320, f32[512]{0:T(512)S(1)} %add_rsqrt_fusion.4, f32[512]{0:T(512)S(1)} %broadcast_multiply_fusion.4, ...), kind=kOutput, calls=%fused_computation.10.clone.1 | convolution fusion | flops 1081344000 | bytes 4732932 | tf_op jit(solution)/shard_map/while/body/eval_jaxpr/dot_general | solution.py:35
  85.0 1.0 copy-done
  86.0 1.3 copy.82
  88.6 0.7 iota_compare_fusion.4
  89.3 5.5 %fusion.74 = (f32[512]{0:T(512)S(1)}, f32[512,4,128]{0,2,1:T(8,128)S(1)}) fusion(f32[512,4,128]{0,2,1:T(8,128)S(1)} %bitcast.71, f32[512,4]{0,1:T(4,128)S(1)} %fusion.73, bf16[1024,4,128]{0,2,1:T(8,128)(2,1)} %get-tuple-element.324, pred[1024]{0:T(1024)(128)(4,1)S(1)} %iota_compare_fusion.4, bf16[1024,4,128]{2,0,1:T(8,128)(2,1)} %get-tuple-element.323, ...), kind=kOutput, calls=%fused_computation.90.clone.1 | convolution fusion | flops 1089207808 | bytes 4729856 | tf_op jit(solution)/shard_map/while/body/eval_jaxpr/hrj,jhd->rhd/dot_general | solution.py:50
  95.3 0.7 add_compare_fusion.2
  96.0 2.5 %fusion.75 = bf16[4,512,512]{2,1,0:T(8,128)(2,1)} fusion(bf16[4,512,512]{2,1,0:T(8,128)(2,1)} %get-tuple-element.299, s32[]{:T(128)S(6)} %copy.88, bf16[512,512]{1,0:T(8,128)(2,1)S(1)} %copy-done.3, f32[512,512]{1,0:T(8,128)S(1)} %copy.84, bf16[512,2048]{1,0:T(8,128)(2,1)} %copy-done, f32[512]{0:T(512)S(1)} %get-tuple-element.325, ...), kind=kOutput, calls=%fused_computation.23.clone.1 | convolution fusion | flops 271056896 | bytes 3152392 | tf_op jit(solution)/shard_map/while/body/eval_jaxpr/dot_general | solution.py:58
  98.5 3.6 %gather_fusion = bf16[16,128,512]{2,1,0:T(8,128)(2,1)} fusion(bf16[16,128,512]{2,1,0:T(8,128)(2,1)} %bitcast.77, s32[1024]{0:T(1024)S(1)} %pad_clamp_fusion.2), kind=kCustom, calls=%fused_computation | custom fusion | bytes 4194368 | tf_op jit(solution)/shard_map/gather | solution.py:111
  102.1 4.8 %all-to-all-start = ((bf16[8,2,128,512]{3,2,1,0:T(8,128)(2,1)}), bf16[8,2,128,512]{3,2,1,0:T(8,128)(2,1)S(1)}, u32[]{:S(2)}, u32[]{:S(2)}) async-start(bf16[8,2,128,512]{3,2,1,0:T(8,128)(2,1)} %bitcast.73), calls=%async_computation | async-start | bytes 4194304 | tf_op jit(solution)/shard_map/all_to_all | solution.py:116
  107.3 0.6 scatter_custom_fusion.1
  108.0 0.7 gather_fusion.3
  108.7 0.7 copy.64
  109.4 24.7 %all-to-all-done = bf16[8,2,128,512]{3,2,1,0:T(8,128)(2,1)S(1)} async-done(((bf16[8,2,128,512]{3,2,1,0:T(8,128)(2,1)}), bf16[8,2,128,512]{3,2,1,0:T(8,128)(2,1)S(1)}, u32[]{:S(2)}, u32[]{:S(2)}) %all-to-all-start) | async-done | bytes 2097184 | tf_op jit(solution)/shard_map/all_to_all | solution.py:116
  134.1 7.0 %all-to-all-start.3 = ((s32[16,1,1]{2,1,0:T(1,128)}), s32[16,1,1]{2,1,0:T(1,128)S(1)}, u32[]{:S(2)}, u32[]{:S(2)}) async-start(s32[16,1,1]{2,1,0:T(1,128)} %copy.64), calls=%async_computation.3 | async-start | bytes 16384 | tf_op jit(solution)/shard_map/all_to_all | solution.py:126
  141.1 2.0 %gather_fusion.2 = bf16[16,128,512]{2,1,0:T(8,128)(2,1)} fusion(bf16[16,128,512]{2,1,0:T(8,128)(2,1)S(1)} %bitcast.72, s32[1024]{0:T(1024)S(1)} %pad_clamp_fusion.1), kind=kCustom, calls=%fused_computation.2 | custom fusion | bytes 4194368 | tf_op jit(solution)/shard_map/gather | solution.py:122
  143.1 5.6 %all-to-all-done.3 = s32[16,1,1]{2,1,0:T(1,128)S(1)} async-done(((s32[16,1,1]{2,1,0:T(1,128)}), s32[16,1,1]{2,1,0:T(1,128)S(1)}, u32[]{:S(2)}, u32[]{:S(2)}) %all-to-all-start.3) | async-done | bytes 96 | tf_op jit(solution)/shard_map/all_to_all | solution.py:126
  148.7 3.7 %all-to-all-start.2 = ((bf16[16,1,128,512]{3,2,1,0:T(8,128)(2,1)}), bf16[16,1,128,512]{3,2,1,0:T(8,128)(2,1)S(1)}, u32[]{:S(2)}, u32[]{:S(2)}) async-start(bf16[16,1,128,512]{3,2,1,0:T(8,128)(2,1)} %bitcast.74), calls=%async_computation.2 | async-start | bytes 4194304 | tf_op jit(solution)/shard_map/all_to_all | solution.py:125
  152.8 0.6 scatter_custom_fusion.2
  153.5 27.2 %all-to-all-done.2 = bf16[16,1,128,512]{3,2,1,0:T(8,128)(2,1)S(1)} async-done(((bf16[16,1,128,512]{3,2,1,0:T(8,128)(2,1)}), bf16[16,1,128,512]{3,2,1,0:T(8,128)(2,1)S(1)}, u32[]{:S(2)}, u32[]{:S(2)}) %all-to-all-start.2) | async-done | bytes 2097184 | tf_op jit(solution)/shard_map/all_to_all | solution.py:125
  180.7 2.0 %gather_fusion.4 = bf16[16,128,512]{2,1,0:T(8,128)(2,1)} fusion(bf16[16,128,512]{2,1,0:T(8,128)(2,1)S(1)} %bitcast.75, s32[1024]{0:T(1024)S(1)} %pad_clamp_fusion), kind=kCustom, calls=%fused_computation.4 | custom fusion | bytes 4194368 | tf_op jit(solution)/shard_map/gather | solution.py:135
  (101 shorter events, 9.0 us)
Async XLA Ops:
  3.7 98.5 %all-to-all-start.1 = ((s32[8,2,2]{1,2,0:T(2,128)}), s32[8,2,2]{1,2,0:T(2,128)S(1)}, u32[]{:S(2)}, u32[]{:S(2)}) async-start(s32[8,2,2]{1,2,0:T(2,128)} %copy.62), calls=%async_computation.1 | async-start | bytes 16384 | tf_op jit(solution)/shard_map/all_to_all | solution.py:117
  9.1 3.0 %copy-start.2 = (bf16[1,1024,512]{2,1,0:T(8,128)(2,1)S(1)}, bf16[1,1024,512]{2,1,0:T(8,128)(2,1)}, u32[]{:S(2)}) copy-start(bf16[1,1024,512]{2,1,0:T(8,128)(2,1)} %param.16) | copy-start | bytes 3145732
  10.7 2.7 %copy-start.4 = (f32[2048]{0:T(1024)S(1)}, f32[2048]{0:T(1024)}, u32[]{:S(2)}) copy-start(f32[2048]{0:T(1024)} %param.23) | copy-start | bytes 24580
  10.7 2.7 %copy-start.5 = (f32[512]{0:T(512)S(1)}, f32[512]{0:T(512)}, u32[]{:S(2)}) copy-start(f32[512]{0:T(512)} %param.21) | copy-start | bytes 6148
  10.7 2.7 %copy-start.6 = (f32[512]{0:T(512)S(1)}, f32[512]{0:T(512)}, u32[]{:S(2)}) copy-start(f32[512]{0:T(512)} %param.24) | copy-start | bytes 6148
  20.9 1.4 copy-start
  24.0 1.4 copy-start.1
  30.9 1.2 copy-start.3
  42.1 1.4 copy-start
  45.3 1.4 copy-start.1
  52.2 1.2 copy-start.3
  63.4 1.4 copy-start
  66.6 1.4 copy-start.1
  73.5 1.2 copy-start.3
  84.7 1.4 copy-start
  87.8 1.4 copy-start.1
  94.8 1.2 copy-start.3
  102.1 32.0 %all-to-all-start = ((bf16[8,2,128,512]{3,2,1,0:T(8,128)(2,1)}), bf16[8,2,128,512]{3,2,1,0:T(8,128)(2,1)S(1)}, u32[]{:S(2)}, u32[]{:S(2)}) async-start(bf16[8,2,128,512]{3,2,1,0:T(8,128)(2,1)} %bitcast.73), calls=%async_computation | async-start | bytes 4194304 | tf_op jit(solution)/shard_map/all_to_all | solution.py:116
  134.1 14.6 %all-to-all-start.3 = ((s32[16,1,1]{2,1,0:T(1,128)}), s32[16,1,1]{2,1,0:T(1,128)S(1)}, u32[]{:S(2)}, u32[]{:S(2)}) async-start(s32[16,1,1]{2,1,0:T(1,128)} %copy.64), calls=%async_computation.3 | async-start | bytes 16384 | tf_op jit(solution)/shard_map/all_to_all | solution.py:126
  148.7 32.0 %all-to-all-start.2 = ((bf16[16,1,128,512]{3,2,1,0:T(8,128)(2,1)}), bf16[16,1,128,512]{3,2,1,0:T(8,128)(2,1)S(1)}, u32[]{:S(2)}, u32[]{:S(2)}) async-start(bf16[16,1,128,512]{3,2,1,0:T(8,128)(2,1)} %bitcast.74), calls=%async_computation.2 | async-start | bytes 4194304 | tf_op jit(solution)/shard_map/all_to_all | solution.py:125
where the time goes:
time: 184 us; the launch traced here: 183 us
  waiting for transfers between devices  57.5 us (31%)
  matrix products  46.1 us (25%)
  local copies, waits for them, and re-layouts  32.2 us (18%)
  other arithmetic  22.4 us (12%)
  starting transfers between devices  21 us (11%)
  loops' own time  3.34 us (2%)
    all_to_all x1, waiting for transfers between devices, shards(): lax.all_to_all(onward, 'dev', split_axis=0, concat_axis=0, tiled=True)  27.2 us
    all_to_all x1, waiting for transfers between devices, shards(): lax.all_to_all(outgoing, 'grp', split_axis=0, concat_axis=0, tiled=True)  24.7 us
    dot_general x4, matrix products, one_block(): jnp.einsum('hrj,jhd->rhd', weights, prefix_v, preferred_element_type=jnp....  21.9 us
    dot_general x4, matrix products, one_block(): jnp.dot(normed, w_in, preferred_element_type=jnp.float32) + b_in  14.2 us
    dot_general x4, matrix products, one_block(): jnp.dot(gated_rows, w_out, preferred_element_type=jnp.float32)  10 us
    all_to_all x1, starting transfers between devices, shards(): lax.all_to_all(slot_onward, 'dev', split_axis=0, concat_axis=0, tiled=True)  7.03 us
    reduce_sum x8, other arithmetic, normalize(): spread = jnp.mean(centred * centred, axis=-1, keepdims=True)  6.01 us
    all_to_all x1, waiting for transfers between devices, shards(): lax.all_to_all(slot_onward, 'dev', split_axis=0, concat_axis=0, tiled=True)  5.58 us
  transfers between devices with their start and end apart: 4, of which 3 were waited for; matrix products, arithmetic and copies ran while one was open for 50% of the time, Pallas kernels for 0%

commit v1 on v0

v1 whole, which is shorter than its diff:
```python
import functools

import jax
import jax.numpy as jnp
from jax import lax
from jax.experimental import pallas as pl
from jax.experimental.pallas import tpu as pltpu
from jax.sharding import PartitionSpec as P

HEADS = 4
BLK = 128
CHUNKS = 4
KEY_TILE = 256
MESH = pl.DeviceIdType.MESH
F32 = jnp.float32
BF16 = jnp.bfloat16
ORDER_G, ORDER_D, PICK_1, PICK_2, SLOT_1, SLOT_2 = range(6)


def log2(number):
    return number.bit_length() - 1


def lanes(shape):
    return lax.broadcasted_iota(jnp.int32, shape, 1)


def rows_of(shape):
    return lax.broadcasted_iota(jnp.int32, shape, 0)


def stack_rows(ref, count):
    tiles = []
    for first in range(0, count, 8):
        tile = jnp.full((8, 128), -1, jnp.int32)
        for step in range(first, min(first + 8, count)):
            tile = jnp.where(rows_of((8, 128)) == step - first, ref[step], tile)
        tiles.append(tile)
    return tiles[0] if len(tiles) == 1 else jnp.concatenate(tiles, axis=0)


def column(matrix, index):
    return matrix[:, index : index + 1]


def centre(matrix, width):
    average = jnp.sum(matrix, axis=-1, keepdims=True) * (1.0 / width)
    centred = matrix - average
    spread = jnp.sum(centred * centred, axis=-1, keepdims=True) * (1.0 / width)
    return centred * lax.rsqrt(spread + 1e-06)


def half_silu(half):
    return half + half * jnp.tanh(half)


def kernel(sizes, *refs):
    ng, nd, nblk, width, prefix, rows = sizes
    piece = BLK // CHUNKS
    part = piece // 2
    sub = nblk // 2
    tile_rows = sub * piece
    head_dim = width // HEADS
    (
        count_ref,
        length_ref,
        device_ref,
        slot_ref,
        gain_ref,
        bias_ref,
        again_ref,
        cand_hbm,
        key_hbm,
        value_hbm,
        win_hbm,
        wout_hbm,
        out_ref,
        cand,
        keys,
        keys_t,
        values,
        win,
        wout,
        proj,
        res,
        tab_own,
        tab_g,
        tab_d,
        slot_own_1,
        slot_own_2,
        slot_in_1,
        slot_in_2,
        idx_v,
        idx,
        load_sem,
        idx_sem,
        meta_send,
        meta_recv,
        data_send,
        data_recv,
        *bufs,
    ) = refs
    send_a1, recv_a1, send_b1, recv_b1, send_a2, recv_a2, send_b2, recv_b2 = (
        bufs[CHUNKS * k : CHUNKS * (k + 1)] for k in range(8)
    )
    me_g = lax.axis_index("grp")
    me_d = lax.axis_index("dev")

    def at_group(step):
        return {"grp": (me_g + step) & (ng - 1), "dev": me_d}

    def at_member(step):
        return {"grp": me_g, "dev": (me_d + step) & (nd - 1)}

    loads = [
        pltpu.make_async_copy(src, dst, load_sem.at[k])
        for k, (src, dst) in enumerate(
            (
                (cand_hbm, cand),
                (win_hbm, win),
                (key_hbm, keys),
                (value_hbm, values),
                (wout_hbm, wout),
            )
        )
    ]
    for load in loads:
        load.start()

    barrier = pltpu.get_barrier_semaphore()

    def greet_group(step, carry):
        pl.semaphore_signal(barrier, inc=1, device_id=at_group(step), device_id_type=MESH)
        return carry

    def greet_member(step, carry):
        pl.semaphore_signal(barrier, inc=1, device_id=at_member(step), device_id_type=MESH)
        return carry

    lax.fori_loop(1, ng, greet_group, 0)
    lax.fori_loop(1, nd, greet_member, 0)

    def own_table():
        tab_own[...] = jnp.full((8, 128), -1, jnp.int32)
        code = device_ref[...] * nblk + slot_ref[...]
        tab_own[:, 0:nblk] = jnp.broadcast_to(code, (8, nblk))
        table = tab_own[...]
        device = lax.shift_right_arithmetic(table, log2(nblk))
        group = lax.shift_right_arithmetic(device, log2(nd))
        member = jnp.where(table < 0, -1, device & (nd - 1))
        lane = lanes((8, 128))
        live = lane < nblk
        want_g = jnp.where(
            live, (me_g + lax.shift_right_arithmetic(lane, 1)) & (ng - 1), -7
        )
        want_d = jnp.where(live, (me_d + lane) & (nd - 1), -7)
        low = jnp.full((8, 128), nblk - 1, jnp.int32)
        high = jnp.zeros((8, 128), jnp.int32)
        order_d = jnp.zeros((8, 128), jnp.int32)
        for i in range(nblk):
            hit_g = column(group, i) == want_g
            low = jnp.where(hit_g, jnp.minimum(low, i), low)
            high = jnp.where(hit_g, jnp.maximum(high, i), high)
            order_d = jnp.where(column(member, i) == want_d, i, order_d)
        order_g = jnp.where((lane & 1) == 0, low, high)
        row = rows_of((8, 128))
        idx_v[...] = jnp.where(
            row == ORDER_G, order_g, jnp.where(row == ORDER_D, order_d, 0)
        )
        tab_g[0] = table
        tab_d[0] = table

    def publish():
        copy = pltpu.make_async_copy(idx_v, idx, idx_sem)
        copy.start()
        copy.wait()

    def send_tables():
        def to_group(step, carry):
            pltpu.make_async_remote_copy(
                tab_own, tab_g.at[step], meta_send.at[0], meta_recv.at[0], at_group(step), MESH
            ).start()
            return carry

        def to_member(step, carry):
            pltpu.make_async_remote_copy(
                tab_own, tab_d.at[step], meta_send.at[1], meta_recv.at[1], at_member(step), MESH
            ).start()
            return carry

        lax.fori_loop(1, ng, to_group, 0)
        lax.fori_loop(1, nd, to_member, 0)

    def wait_bytes(sem, ref):
        pltpu.make_async_copy(ref, ref, sem).wait()

    def middle_tables():
        wait_bytes(meta_recv.at[0], tab_g.at[pl.ds(1, ng - 1)])
        wait_bytes(meta_recv.at[1], tab_d.at[pl.ds(1, nd - 1)])
        table = stack_rows(tab_g, ng)
        shape = table.shape
        device = lax.shift_right_arithmetic(table, log2(nblk))
        group = lax.shift_right_arithmetic(device, log2(nd))
        slot = table & (nblk - 1)
        lane = lanes(shape)
        mine = group == me_g
        first = jnp.min(
            jnp.where(mine, lane.astype(F32), 1000.0), axis=1, keepdims=True
        ).astype(jnp.int32)
        place = 2 * rows_of(shape) + jnp.where(lane > first, 1, 0)
        both = place * nblk + slot
        want = jnp.where(lane < nblk, me_g * nd + ((me_d + lane) & (nd - 1)), -7)
        found = jnp.zeros(shape, jnp.int32)
        for i in range(nblk):
            found = found + jnp.where(column(device, i) == want, column(both, i), 0)
        found = jnp.sum(found, axis=0, keepdims=True)
        found = jnp.broadcast_to(found, (8, 128))
        pick_1 = lax.shift_right_arithmetic(found, log2(nblk))
        slot_own_1[...] = found & (nblk - 1)
        table = stack_rows(tab_d, nd)
        shape = table.shape
        device = lax.shift_right_arithmetic(table, log2(nblk))
        both = rows_of(shape) * nblk + (table & (nblk - 1))
        lane = lanes(shape)
        want = jnp.where(
            lane < nblk,
            ((me_g + lax.shift_right_arithmetic(lane, 1)) & (ng - 1)) * nd + me_d,
            -7,
        )
        top = nd * nblk - 1
        low = jnp.full(shape, top, jnp.int32)
        high = jnp.zeros(shape, jnp.int32)
        for i in range(nblk):
            hit = column(device, i) == want
            low = jnp.where(hit, jnp.minimum(low, column(both, i)), low)
            high = jnp.where(hit, jnp.maximum(high, column(both, i)), high)
        low = jnp.broadcast_to(jnp.min(low, axis=0, keepdims=True), (8, 128))
        high = jnp.broadcast_to(jnp.max(high, axis=0, keepdims=True), (8, 128))
        found = jnp.where((lanes((8, 128)) & 1) == 0, low, high)
        pick_2 = lax.shift_right_arithmetic(found, log2(nblk))
        slot_own_2[...] = found & (nblk - 1)
        row = rows_of((8, 128))
        idx_v[...] = jnp.where(
            row == PICK_1, pick_1, jnp.where(row == PICK_2, pick_2, idx_v[...])
        )
        slot_in_1[0] = slot_own_1[...]
        slot_in_2[0] = slot_own_2[...]

        def to_member(step, carry):
            pltpu.make_async_remote_copy(
                slot_own_1, slot_in_1.at[step], meta_send.at[2], meta_recv.at[2],
                at_member(step), MESH,
            ).start()
            return carry

        def to_group(step, carry):
            pltpu.make_async_remote_copy(
                slot_own_2, slot_in_2.at[step], meta_send.at[3], meta_recv.at[3],
                at_group(step), MESH,
            ).start()
            return carry

        lax.fori_loop(1, nd, to_member, 0)
        lax.fori_loop(1, ng, to_group, 0)
        publish()

    def final_tables():
        wait_bytes(meta_recv.at[2], slot_in_1.at[pl.ds(1, nd - 1)])
        wait_bytes(meta_recv.at[3], slot_in_2.at[pl.ds(1, ng - 1)])

        def place(table, lane_of_row, number):
            lane, row = lanes(table.shape), rows_of(table.shape)
            slot = jnp.sum(
                jnp.where(lane == lane_of_row(row), table, 0).astype(F32), axis=1, keepdims=True
            ).astype(jnp.int32)
            slot = jnp.where(column(row, 0) < number, slot, -7)
            hit = jnp.where(slot == lane, lane_of_row(row), 0)
            return jnp.broadcast_to(jnp.sum(hit, axis=0, keepdims=True), (8, 128))

        table = stack_rows(slot_in_1, nd)
        slot_1 = place(table, lambda row: row, nd)
        table = stack_rows(slot_in_2, ng)
        slot_2 = place(table, lambda row: 2 * row, ng) + place(table, lambda row: 2 * row + 1, ng)
        row = rows_of((8, 128))
        idx_v[...] = jnp.where(
            row == SLOT_1, slot_1, jnp.where(row == SLOT_2, slot_2, idx_v[...])
        )
        publish()

    def look(row, lane):
        return idx[row, lane] & (nblk - 1)

    def remote(src, dst, kind, c, where):
        return pltpu.make_async_remote_copy(
            src, dst, data_send.at[kind, c], data_recv.at[kind, c], where, MESH
        )

    def send_first(c):
        for k in range(2):
            recv_a1[c][k] = res[look(ORDER_G, k), 0:part, :]
        recv_a2[c][0] = res[look(ORDER_D, 0), part:piece, :]

        def group_step(step, carry):
            for k in range(2):
                send_a1[c][2 * step + k] = res[look(ORDER_G, 2 * step + k), 0:part, :]
            span = pl.ds(2 * step, 2)
            remote(send_a1[c].at[span], recv_a1[c].at[span], 0, c, at_group(step)).start()
            return carry

        def member_step(step, carry):
            send_a2[c][step] = res[look(ORDER_D, step), part:piece, :]
            remote(send_a2[c].at[step], recv_a2[c].at[step], 1, c, at_member(step)).start()
            return carry

        lax.fori_loop(1, ng, group_step, 0)
        lax.fori_loop(1, nd, member_step, 0)

    def send_second(c):
        wait_bytes(data_recv.at[0, c], recv_a1[c].at[pl.ds(2, nblk - 2)])
        recv_b1[c][0] = recv_a1[c][look(PICK_1, 0)]

        def member_step(step, carry):
            send_b1[c][step] = recv_a1[c][look(PICK_1, step)]
            remote(send_b1[c].at[step], recv_b1[c].at[step], 2, c, at_member(step)).start()
            return carry

        lax.fori_loop(1, nd, member_step, 0)
        wait_bytes(data_recv.at[1, c], recv_a2[c].at[pl.ds(1, nd - 1)])
        for k in range(2):
            recv_b2[c][k] = recv_a2[c][look(PICK_2, k)]

        def group_step(step, carry):
            for k in range(2):
                send_b2[c][2 * step + k] = recv_a2[c][look(PICK_2, 2 * step + k)]
            span = pl.ds(2 * step, 2)
            remote(send_b2[c].at[span], recv_b2[c].at[span], 3, c, at_group(step)).start()
            return carry

        lax.fori_loop(1, ng, group_step, 0)

    def deliver(c):
        wait_bytes(data_recv.at[2, c], recv_b1[c].at[pl.ds(1, nd - 1)])
        wait_bytes(data_recv.at[3, c], recv_b2[c].at[pl.ds(2, nblk - 2)])

        def slot_step(s, carry):
            out_ref[s, c * piece : c * piece + part, :] = recv_b1[c][look(SLOT_1, s)]
            out_ref[s, c * piece + part : (c + 1) * piece, :] = recv_b2[c][look(SLOT_2, s)]
            return carry

        lax.fori_loop(0, nblk, slot_step, 0)

    def prepare_prefix():
        loads[2].wait()
        loads[3].wait()
        live = length_ref[0]
        for first in range(0, prefix, KEY_TILE):
            span = slice(first, first + KEY_TILE)
            keys_t[:, span] = keys[span, :].T
            shape = (KEY_TILE, width)
            values[span, :] = jnp.where(
                rows_of(shape) + first < live, values[span, :], jnp.zeros(shape, BF16)
            )

    score_scale = 0.5 / (head_dim**0.5)

    def compute(t):
        c = lax.shift_right_logical(t, 1)
        first_block = pl.multiple_of((t & 1) * sub, sub)
        first_row = pl.multiple_of(c * piece, piece)

        @pl.when(t == 0)
        def _():
            loads[0].wait()
            loads[1].wait()

        x = cand[pl.ds(first_block, sub), pl.ds(first_row, piece), :]
        x = x.reshape(tile_rows, width).astype(F32)
        normed = (centre(x, width) * (gain_ref[...] * 0.5)).astype(BF16)
        step_cols = 256
        for first in range(0, 4 * width, step_cols):
            span = slice(first, first + step_cols)
            half = jnp.dot(normed, win[:, span], preferred_element_type=F32)
            act = half_silu(half + bias_ref[:, span] * 0.5)
            if 2 * width <= first < 3 * width:
                act = act * score_scale
            proj[:, span] = act.astype(BF16)

        @pl.when(t == 0)
        def _():
            prepare_prefix()
            loads[4].wait()

        heads = []
        for h in range(HEADS):
            cols = slice(h * head_dim, (h + 1) * head_dim)
            query = proj[:, 2 * width + h * head_dim : 2 * width + (h + 1) * head_dim]
            own_key = proj[:, 3 * width + h * head_dim : 3 * width + (h + 1) * head_dim]
            own_value = proj[:, width + h * head_dim : width + (h + 1) * head_dim]
            total = None
            for first in range(0, prefix, KEY_TILE):
                span = slice(first, first + KEY_TILE)
                half = jnp.dot(query, keys_t[cols, span], preferred_element_type=F32)
                weights = half_silu(half).astype(BF16)
                term = jnp.dot(weights, values[span, cols], preferred_element_type=F32)
                total = term if total is None else total + term
            own = jnp.sum(query.astype(F32) * own_key.astype(F32), axis=-1, keepdims=True)
            own = half_silu(own).astype(BF16).astype(F32)
            heads.append(total + own * own_value.astype(F32))
        attended = jnp.concatenate(heads, axis=1)
        gated = (
            centre(attended, width) * again_ref[...] * proj[:, 0:width].astype(F32)
        ).astype(BF16)
        x = cand[pl.ds(first_block, sub), pl.ds(first_row, piece), :]
        x = x.reshape(tile_rows, width).astype(F32)
        layer_out = x + jnp.dot(gated, wout[...], preferred_element_type=F32)
        shape = (sub, piece, width)
        row = (
            (lax.broadcasted_iota(jnp.int32, shape, 0) + first_block) * BLK
            + lax.broadcasted_iota(jnp.int32, shape, 1)
            + first_row
        )
        layer_out = jnp.where(row < count_ref[0], layer_out.reshape(shape), 0.0)
        res[pl.ds(first_block, sub), :, :] = layer_out.astype(BF16)

    own_table()
    publish()

    def step(t, carry):
        compute(t)

        @pl.when(t == 0)
        def _():
            pl.semaphore_wait(barrier, ng + nd - 2)
            send_tables()

        for c in range(CHUNKS):

            @pl.when(t == 2 * c + 1)
            def _():
                send_first(c)
                if c == 1:
                    middle_tables()
                if c >= 1:
                    send_second(c - 1)
                if c == 2:
                    final_tables()
                if c >= 2:
                    deliver(c - 2)

        return carry

    lax.fori_loop(0, 2 * CHUNKS, step, 0)
    last = CHUNKS - 1
    send_second(last)
    deliver(last - 1)
    deliver(last)

    wait_bytes(meta_send.at[0], tab_g.at[pl.ds(1, ng - 1)])
    wait_bytes(meta_send.at[1], tab_d.at[pl.ds(1, nd - 1)])
    wait_bytes(meta_send.at[2], slot_in_1.at[pl.ds(1, nd - 1)])
    wait_bytes(meta_send.at[3], slot_in_2.at[pl.ds(1, ng - 1)])
    for c in range(CHUNKS):
        wait_bytes(data_send.at[0, c], send_a1[c].at[pl.ds(2, nblk - 2)])
        wait_bytes(data_send.at[1, c], send_a2[c].at[pl.ds(1, nd - 1)])
        wait_bytes(data_send.at[2, c], send_b1[c].at[pl.ds(1, nd - 1)])
        wait_bytes(data_send.at[3, c], send_b2[c].at[pl.ds(2, nblk - 2)])


def layer(
    ng,
    nd,
    candidates,
    prefix_keys,
    prefix_values,
    cand_count,
    prefix_len,
    dest_device,
    dest_slot,
    norm_gain,
    w_in,
    b_in,
    attn_gain,
    w_out,
):
    rows, width = candidates.shape
    prefix = prefix_keys.shape[1]
    nblk = rows // BLK
    part = BLK // CHUNKS // 2
    tile_rows = nblk // 2 * (BLK // CHUNKS)
    smem = pl.BlockSpec(memory_space=pltpu.SMEM)
    vmem = pl.BlockSpec(memory_space=pltpu.VMEM)
    hbm = pl.BlockSpec(memory_space=pl.ANY)
    block = pltpu.VMEM((nblk, part, width), BF16)
    table = pltpu.VMEM((8, 128), jnp.int32)
    out = pl.pallas_call(
        functools.partial(kernel, (ng, nd, nblk, width, prefix, rows)),
        out_shape=jax.ShapeDtypeStruct((nblk, BLK, width), BF16),
        in_specs=[smem, smem, vmem, vmem, vmem, vmem, vmem, hbm, hbm, hbm, hbm, hbm],
        out_specs=vmem,
        scratch_shapes=[
            pltpu.VMEM((nblk, BLK, width), BF16),
            pltpu.VMEM((prefix, width), BF16),
            pltpu.VMEM((width, prefix), BF16),
            pltpu.VMEM((prefix, width), BF16),
            pltpu.VMEM((width, 4 * width), BF16),
            pltpu.VMEM((width, width), BF16),
            pltpu.VMEM((tile_rows, 4 * width), BF16),
            pltpu.VMEM((nblk, BLK // CHUNKS, width), BF16),
            table,
            pltpu.VMEM((ng, 8, 128), jnp.int32),
            pltpu.VMEM((nd, 8, 128), jnp.int32),
            table,
            table,
            pltpu.VMEM((nd, 8, 128), jnp.int32),
            pltpu.VMEM((ng, 8, 128), jnp.int32),
            table,
            pltpu.SMEM((8, 128), jnp.int32),
            pltpu.SemaphoreType.DMA((5,)),
            pltpu.SemaphoreType.DMA,
            pltpu.SemaphoreType.DMA((4,)),
            pltpu.SemaphoreType.DMA((4,)),
            pltpu.SemaphoreType.DMA((4, CHUNKS)),
            pltpu.SemaphoreType.DMA((4, CHUNKS)),
        ]
        + [block] * (8 * CHUNKS),
        compiler_params=pltpu.CompilerParams(
            collective_id=0, has_side_effects=True, vmem_limit_bytes=60 * 2**20
        ),
    )(
        cand_count,
        prefix_len,
        dest_device.reshape(1, nblk),
        dest_slot.reshape(1, nblk),
        norm_gain.reshape(1, width),
        b_in.reshape(1, 4 * width),
        attn_gain.reshape(1, width),
        candidates.reshape(nblk, BLK, width),
        prefix_keys[0],
        prefix_values[0],
        w_in,
        w_out,
    )
    return out.reshape(rows, width)


def solution(mesh):
    spec = P(("grp", "dev"))
    wide = P(("grp", "dev"), None)
    deep = P(("grp", "dev"), None, None)
    return jax.shard_map(
        functools.partial(layer, mesh.shape["grp"], mesh.shape["dev"]),
        mesh=mesh,
        in_specs=(wide, deep, deep, spec, spec, spec, spec, P(), P(), P(), P(), P()),
        out_specs=wide,
        check_vma=False,
    )
```

time: 184 us -> 58.8 us (0.32)
  the two profiles are of different devices: /device:TPU:0 before, /device:TPU:1 now
where the time goes in v1:
time: 58.8 us; the launch traced here: 58.2 us
  Pallas kernels  53.8 us (91%)
  local copies, waits for them, and re-layouts  3.05 us (5%)
  between operations  1.3 us (2%)
    pallas_call x1, Pallas kernels, layer(): pl.pallas_call(functools.partial(kernel, (ng, nd, nblk, width, prefix, ro...  53.8 us
    unnamed x1, local copies, waits for them, and re-layouts  3.05 us

profile of v1, /device:TPU:1, one launch (start us, length us, event | category | flops | bytes accessed | tf_op | source)
XLA Modules:
  0.0 58.2 jit_solution(3632646068796704984)
XLA Ops:
  1.3 53.8 %shard_map.118 = bf16[16,128,512]{2,1,0:T(8,128)(2,1)} custom-call(s32[1]{0:T(128)S(6)} %copy.14.refs_0_, s32[1]{0:T(128)S(6)} %copy.15.refs_1_, s32[1,16]{1,0:T(1,128)} %bitcast.16, s32[1,16]{1,0:T(1,128)} %bitcast.17, f32[1,512]{1,0:T(1,128)} %bitcast.14, f32[1,2048]{1,0:T(1,128)} %bitcast.13, f32[1,512]{1,0:T(1,128)} %bitcast.15, ...), custom_call_target="tpu_custom_call" | custom-call | tf_op jit(solution)/shard_map/pallas_call | solution.py:495
  55.1 3.0 %copy.16 = bf16[2048,512]{1,0:T(8,128)(2,1)} copy(bf16[2048,512]{1,0:T(8,128)(2,1)} %bitcast.9) | data formatting | bytes 4194304

commit v2 on v1

--- a/solution.py
+++ b/solution.py
@@ -9,8 +9,12 @@
 
 HEADS = 4
 BLK = 128
-CHUNKS = 4
+CHUNKS = 8
+LAG = 4
+LAST_LAG = 7
 KEY_TILE = 256
+AHEAD = 2
+COLS = 256
 MESH = pl.DeviceIdType.MESH
 F32 = jnp.float32
 BF16 = jnp.bfloat16
@@ -55,13 +59,24 @@
 
 
 def kernel(sizes, *refs):
-    ng, nd, nblk, width, prefix, rows = sizes
+    ng, nd, nblk, width, prefix = sizes
     piece = BLK // CHUNKS
-    part = piece // 2
-    sub = nblk // 2
-    tile_rows = sub * piece
+    tile_rows = nblk * piece
     head_dim = width // HEADS
     (
+        count_hbm,
+        length_hbm,
+        device_hbm,
+        slot_hbm,
+        gain_hbm,
+        bias_hbm,
+        again_hbm,
+        cand_hbm,
+        key_hbm,
+        value_hbm,
+        win_hbm,
+        wout_hbm,
+        out_ref,
         count_ref,
         length_ref,
         device_ref,
@@ -69,20 +84,17 @@
         gain_ref,
         bias_ref,
         again_ref,
-        cand_hbm,
-        key_hbm,
-        value_hbm,
-        win_hbm,
-        wout_hbm,
-        out_ref,
+        cand_first,
         cand,
         keys,
         keys_t,
         values,
         win,
         wout,
-        proj,
-        res,
+        nrm,
+        gate,
+        qkv,
+        att,
         tab_own,
         tab_g,
         tab_d,
@@ -100,9 +112,7 @@
         data_recv,
         *bufs,
     ) = refs
-    send_a1, recv_a1, send_b1, recv_b1, send_a2, recv_a2, send_b2, recv_b2 = (
-        bufs[CHUNKS * k : CHUNKS * (k + 1)] for k in range(8)
-    )
+    send_a, recv_a, send_b, recv_b = (bufs[CHUNKS * k : CHUNKS * (k + 1)] for k in range(4))
     me_g = lax.axis_index("grp")
     me_d = lax.axis_index("dev")
 
@@ -112,14 +122,36 @@
     def at_member(step):
         return {"grp": me_g, "dev": (me_d + step) & (nd - 1)}
 
-    loads = [
+    (
+        load_device,
+        load_slot,
+        load_gain,
+        load_bias,
+        load_again,
+        load_count,
+        load_length,
+        load_first,
+        load_win,
+        load_keys,
+        load_values,
+        load_cand,
+        load_wout,
+    ) = loads = [
         pltpu.make_async_copy(src, dst, load_sem.at[k])
         for k, (src, dst) in enumerate(
             (
-                (cand_hbm, cand),
+                (device_hbm, device_ref),
+                (slot_hbm, slot_ref),
+                (gain_hbm, gain_ref),
+                (bias_hbm, bias_ref),
+                (again_hbm, again_ref),
+                (count_hbm, count_ref),
+                (length_hbm, length_ref),
+                (cand_hbm.at[:, pl.ds(0, piece), :], cand_first),
                 (win_hbm, win),
                 (key_hbm, keys),
                 (value_hbm, values),
+                (cand_hbm, cand),
                 (wout_hbm, wout),
             )
         )
@@ -290,72 +322,70 @@
     def look(row, lane):
         return idx[row, lane] & (nblk - 1)
 
-    def remote(src, dst, kind, c, where):
+    def remote(src, dst, stage, c, where):
         return pltpu.make_async_remote_copy(
-            src, dst, data_send.at[kind, c], data_recv.at[kind, c], where, MESH
+            src, dst, data_send.at[stage, c], data_recv.at[stage, c], where, MESH
         )
 
+    def to_groups(src, dst, stage, c):
+        def step(number, carry):
+            span = pl.ds(2 * number, 2)
+            remote(src.at[span], dst.at[span], stage, c, at_group(number)).start()
+            return carry
+
+        lax.fori_loop(1, ng, step, 0)
+
+    def to_members(src, dst, stage, c):
+        def step(number, carry):
+            remote(src.at[number], dst.at[number], stage, c, at_member(number)).start()
+            return carry
+
+        lax.fori_loop(1, nd, step, 0)
+
+    def far(ref, by_group):
+        return ref.at[pl.ds(2, nblk - 2)] if by_group else ref.at[pl.ds(1, nd - 1)]
+
     def send_first(c):
-        for k in range(2):
-            recv_a1[c][k] = res[look(ORDER_G, k), 0:part, :]
-        recv_a2[c][0] = res[look(ORDER_D, 0), part:piece, :]
-
-        def group_step(step, carry):
-            for k in range(2):
-                send_a1[c][2 * step + k] = res[look(ORDER_G, 2 * step + k), 0:part, :]
-            span = pl.ds(2 * step, 2)
-            remote(send_a1[c].at[span], recv_a1[c].at[span], 0, c, at_group(step)).start()
-            return carry
-
-        def member_step(step, carry):
-            send_a2[c][step] = res[look(ORDER_D, step), part:piece, :]
-            remote(send_a2[c].at[step], recv_a2[c].at[step], 1, c, at_member(step)).start()
-            return carry
-
-        lax.fori_loop(1, ng, group_step, 0)
-        lax.fori_loop(1, nd, member_step, 0)
+        (to_groups if c % 2 else to_members)(send_a[c], recv_a[c], 0, c)
 
     def send_second(c):
-        wait_bytes(data_recv.at[0, c], recv_a1[c].at[pl.ds(2, nblk - 2)])
-        recv_b1[c][0] = recv_a1[c][look(PICK_1, 0)]
-
-        def member_step(step, carry):
-            send_b1[c][step] = recv_a1[c][look(PICK_1, step)]
-            remote(send_b1[c].at[step], recv_b1[c].at[step], 2, c, at_member(step)).start()
-            return carry
-
-        lax.fori_loop(1, nd, member_step, 0)
-        wait_bytes(data_recv.at[1, c], recv_a2[c].at[pl.ds(1, nd - 1)])
-        for k in range(2):
-            recv_b2[c][k] = recv_a2[c][look(PICK_2, k)]
-
-        def group_step(step, carry):
-            for k in range(2):
-                send_b2[c][2 * step + k] = recv_a2[c][look(PICK_2, 2 * step + k)]
-            span = pl.ds(2 * step, 2)
-            remote(send_b2[c].at[span], recv_b2[c].at[span], 3, c, at_group(step)).start()
-            return carry
-
-        lax.fori_loop(1, ng, group_step, 0)
+        wait_bytes(data_recv.at[0, c], far(recv_a[c], c % 2))
+        near = 1 if c % 2 else 2
+        pick = PICK_1 if c % 2 else PICK_2
+        for k in range(near):
+            recv_b[c][k] = recv_a[c][look(pick, k)]
+
+        def step(number, carry):
+            for k in range(near):
+                send_b[c][near * number + k] = recv_a[c][look(pick, near * number + k)]
+            span = pl.ds(near * number, near)
+            where = at_member(number) if c % 2 else at_group(number)
+            remote(send_b[c].at[span], recv_b[c].at[span], 1, c, where).start()
+            return carry
+
+        lax.fori_loop(1, nblk // near, step, 0)
 
     def deliver(c):
-        wait_bytes(data_recv.at[2, c], recv_b1[c].at[pl.ds(1, nd - 1)])
-        wait_bytes(data_recv.at[3, c], recv_b2[c].at[pl.ds(2, nblk - 2)])
-
-        def slot_step(s, carry):
-            out_ref[s, c * piece : c * piece + part, :] = recv_b1[c][look(SLOT_1, s)]
-            out_ref[s, c * piece + part : (c + 1) * piece, :] = recv_b2[c][look(SLOT_2, s)]
-            return carry
-
-        lax.fori_loop(0, nblk, slot_step, 0)
+        wait_bytes(data_recv.at[1, c], far(recv_b[c], c % 2 == 0))
+
+        def step(number, carry):
+            for s in (2 * number, 2 * number + 1):
+                slot = look(SLOT_1 if c % 2 else SLOT_2, s)
+                out_ref[s, c * piece : (c + 1) * piece, :] = recv_b[c][slot]
+            return carry
+
+        lax.fori_loop(0, nblk // 2, step, 0)
 
     def prepare_prefix():
-        loads[2].wait()
-        loads[3].wait()
+        load_keys.wait()
+        for first in range(0, prefix, KEY_TILE):
+            span = slice(first, first + KEY_TILE)
+            keys_t[:, span] = keys[span, :].T
+        load_values.wait()
+        load_length.wait()
         live = length_ref[0]
         for first in range(0, prefix, KEY_TILE):
             span = slice(first, first + KEY_TILE)
-            keys_t[:, span] = keys[span, :].T
             shape = (KEY_TILE, width)
             values[span, :] = jnp.where(
                 rows_of(shape) + first < live, values[span, :], jnp.zeros(shape, BF16)
@@ -363,107 +393,155 @@
 
     score_scale = 0.5 / (head_dim**0.5)
 
-    def compute(t):
-        c = lax.shift_right_logical(t, 1)
-        first_block = pl.multiple_of((t & 1) * sub, sub)
-        first_row = pl.multiple_of(c * piece, piece)
-
-        @pl.when(t == 0)
-        def _():
-            loads[0].wait()
-            loads[1].wait()
-
-        x = cand[pl.ds(first_block, sub), pl.ds(first_row, piece), :]
-        x = x.reshape(tile_rows, width).astype(F32)
-        normed = (centre(x, width) * (gain_ref[...] * 0.5)).astype(BF16)
-        step_cols = 256
-        for first in range(0, 4 * width, step_cols):
-            span = slice(first, first + step_cols)
-            half = jnp.dot(normed, win[:, span], preferred_element_type=F32)
-            act = half_silu(half + bias_ref[:, span] * 0.5)
+    def order_of(t):
+        return jnp.where(t % 2 == 1, ORDER_G, ORDER_D)
+
+    def rows_in_order(ref, t, first_row):
+        row = order_of(t)
+        parts = [
+            ref[look(row, place), pl.ds(first_row, piece), :] for place in range(nblk)
+        ]
+        return jnp.concatenate(parts, axis=0).astype(F32)
+
+    def normalise_rows(ref, t, first_row):
+        x = rows_in_order(ref, t, first_row)
+        nrm[...] = (centre(x, width) * (gain_ref[...] * 0.5)).astype(BF16)
+
+    def project(first):
+        half = jnp.dot(nrm[...], win[:, first : first + COLS], preferred_element_type=F32)
+        return half_silu(half + bias_ref[:, first : first + COLS] * 0.5)
+
+    def project_qkv():
+        for first in range(width, 4 * width, COLS):
+            act = project(first)
             if 2 * width <= first < 3 * width:
                 act = act * score_scale
-            proj[:, span] = act.astype(BF16)
-
-        @pl.when(t == 0)
-        def _():
-            prepare_prefix()
-            loads[4].wait()
-
-        heads = []
-        for h in range(HEADS):
+            qkv[:, first - width : first - width + COLS] = act.astype(BF16)
+
+    def attend(following):
+        for first in range(0, width, COLS):
+            gate[:, first : first + COLS] = project(first).astype(BF16)
+        tiles = [(h, first) for h in range(HEADS) for first in range(0, prefix, KEY_TILE)]
+
+        def part_of(group, h):
+            first = group * width + h * head_dim
+            return qkv[:, first : first + head_dim]
+
+        def score(tile):
+            h, first = tile
             cols = slice(h * head_dim, (h + 1) * head_dim)
-            query = proj[:, 2 * width + h * head_dim : 2 * width + (h + 1) * head_dim]
-            own_key = proj[:, 3 * width + h * head_dim : 3 * width + (h + 1) * head_dim]
-            own_value = proj[:, width + h * head_dim : width + (h + 1) * head_dim]
-            total = None
-            for first in range(0, prefix, KEY_TILE):
-                span = slice(first, first + KEY_TILE)
-                half = jnp.dot(query, keys_t[cols, span], preferred_element_type=F32)
-                weights = half_silu(half).astype(BF16)
-                term = jnp.dot(weights, values[span, cols], preferred_element_type=F32)
-                total = term if total is None else total + term
-            own = jnp.sum(query.astype(F32) * own_key.astype(F32), axis=-1, keepdims=True)
-            own = half_silu(own).astype(BF16).astype(F32)
-            heads.append(total + own * own_value.astype(F32))
-        attended = jnp.concatenate(heads, axis=1)
-        gated = (
-            centre(attended, width) * again_ref[...] * proj[:, 0:width].astype(F32)
+            return jnp.dot(
+                part_of(1, h), keys_t[cols, first : first + KEY_TILE], preferred_element_type=F32
+            )
+
+        ahead = [score(tile) for tile in tiles[:AHEAD]]
+        totals = [None] * HEADS
+        for number, (h, first) in enumerate(tiles):
+            half = ahead.pop(0)
+            if number + AHEAD < len(tiles):
+                ahead.append(score(tiles[number + AHEAD]))
+            cols = slice(h * head_dim, (h + 1) * head_dim)
+            weights = half_silu(half).astype(BF16)
+            term = jnp.dot(
+                weights, values[first : first + KEY_TILE, cols], preferred_element_type=F32
+            )
+            totals[h] = term if totals[h] is None else totals[h] + term
+            if first + KEY_TILE == prefix:
+                own = jnp.sum(
+                    part_of(1, h).astype(F32) * part_of(2, h).astype(F32), axis=-1, keepdims=True
+                )
+                own = half_silu(own).astype(BF16).astype(F32)
+                att[:, cols] = totals[h] + own * part_of(0, h).astype(F32)
+                if h == 0 and following is not None:
+                    following()
+
+    def finish_gate():
+        return (
+            centre(att[...], width) * again_ref[...] * gate[...].astype(F32)
         ).astype(BF16)
-        x = cand[pl.ds(first_block, sub), pl.ds(first_row, piece), :]
-        x = x.reshape(tile_rows, width).astype(F32)
-        layer_out = x + jnp.dot(gated, wout[...], preferred_element_type=F32)
-        shape = (sub, piece, width)
-        row = (
-            (lax.broadcasted_iota(jnp.int32, shape, 0) + first_block) * BLK
-            + lax.broadcasted_iota(jnp.int32, shape, 1)
-            + first_row
-        )
-        layer_out = jnp.where(row < count_ref[0], layer_out.reshape(shape), 0.0)
-        res[pl.ds(first_block, sub), :, :] = layer_out.astype(BF16)
-
+
+    def finish(t, gated):
+        first_row = pl.multiple_of(t * piece, piece)
+        delta = jnp.dot(gated, wout[...], preferred_element_type=F32)
+        row = order_of(t)
+        count = count_ref[0]
+        done = []
+        for place in range(nblk):
+            block = look(row, place)
+            x = cand[block, pl.ds(first_row, piece), :].astype(F32)
+            x = x + delta[place * piece : (place + 1) * piece, :]
+            live = rows_of((piece, width)) + (block * BLK + first_row) < count
+            done.append(jnp.where(live, x, 0.0).astype(BF16))
+        return done
+
+    def exchange(t, done):
+        for c in range(CHUNKS):
+
+            @pl.when(t == c)
+            def _():
+                near = 2 if c % 2 else 1
+                for place in range(nblk):
+                    (recv_a[c] if place < near else send_a[c])[place] = done[place]
+                send_first(c)
+                if c == LAG:
+                    middle_tables()
+                if c >= LAG:
+                    send_second(c - LAG)
+                if c == LAST_LAG:
+                    final_tables()
+                if c >= LAST_LAG:
+                    deliver(c - LAST_LAG)
+
+    load_device.wait()
+    load_slot.wait()
     own_table()
     publish()
+    load_first.wait()
+    load_gain.wait()
+    normalise_rows(cand_first, 0, 0)
+    load_bias.wait()
+    load_win.wait()
+    project_qkv()
+    prepare_prefix()
+    load_cand.wait()
+
+    def next_rows(t):
+        normalise_rows(cand, t, pl.multiple_of(t * piece, piece))
+
+    attend(lambda: next_rows(1))
+    load_again.wait()
+    load_count.wait()
+    load_wout.wait()
+    pl.semaphore_wait(barrier, ng + nd - 2)
+    send_tables()
 
     def step(t, carry):
-        compute(t)
-
-        @pl.when(t == 0)
-        def _():
-            pl.semaphore_wait(barrier, ng + nd - 2)
-            send_tables()
-
-        for c in range(CHUNKS):
-
-            @pl.when(t == 2 * c + 1)
-            def _():
-                send_first(c)
-                if c == 1:
-                    middle_tables()
-                if c >= 1:
-                    send_second(c - 1)
-                if c == 2:
-                    final_tables()
-                if c >= 2:
-                    deliver(c - 2)
-
+        gated = finish_gate()
+        project_qkv()
+        done = finish(t - 1, gated)
+        exchange(t - 1, done)
+        attend(lambda: next_rows(jnp.minimum(t + 1, CHUNKS - 1)))
         return carry
 
-    lax.fori_loop(0, 2 * CHUNKS, step, 0)
+    lax.fori_loop(1, CHUNKS, step, 0)
     last = CHUNKS - 1
-    send_second(last)
-    deliver(last - 1)
-    deliver(last)
+    exchange(last, finish(last, finish_gate()))
+    waiting = CHUNKS - LAST_LAG
+    for c in range(CHUNKS - LAG, CHUNKS):
+        send_second(c)
+        if waiting < c - 1:
+            deliver(waiting)
+            waiting += 1
+    for c in range(waiting, CHUNKS):
+        deliver(c)
 
     wait_bytes(meta_send.at[0], tab_g.at[pl.ds(1, ng - 1)])
     wait_bytes(meta_send.at[1], tab_d.at[pl.ds(1, nd - 1)])
     wait_bytes(meta_send.at[2], slot_in_1.at[pl.ds(1, nd - 1)])
     wait_bytes(meta_send.at[3], slot_in_2.at[pl.ds(1, ng - 1)])
     for c in range(CHUNKS):
-        wait_bytes(data_send.at[0, c], send_a1[c].at[pl.ds(2, nblk - 2)])
-        wait_bytes(data_send.at[1, c], send_a2[c].at[pl.ds(1, nd - 1)])
-        wait_bytes(data_send.at[2, c], send_b1[c].at[pl.ds(1, nd - 1)])
-        wait_bytes(data_send.at[3, c], send_b2[c].at[pl.ds(2, nblk - 2)])
+        wait_bytes(data_send.at[0, c], far(send_a[c], c % 2))
+        wait_bytes(data_send.at[1, c], far(send_b[c], c % 2 == 0))
 
 
 def layer(
@@ -485,27 +563,35 @@
     rows, width = candidates.shape
     prefix = prefix_keys.shape[1]
     nblk = rows // BLK
-    part = BLK // CHUNKS // 2
-    tile_rows = nblk // 2 * (BLK // CHUNKS)
-    smem = pl.BlockSpec(memory_space=pltpu.SMEM)
-    vmem = pl.BlockSpec(memory_space=pltpu.VMEM)
+    piece = BLK // CHUNKS
+    tile_rows = nblk * piece
     hbm = pl.BlockSpec(memory_space=pl.ANY)
-    block = pltpu.VMEM((nblk, part, width), BF16)
+    block = pltpu.VMEM((nblk, piece, width), BF16)
     table = pltpu.VMEM((8, 128), jnp.int32)
     out = pl.pallas_call(
-        functools.partial(kernel, (ng, nd, nblk, width, prefix, rows)),
+        functools.partial(kernel, (ng, nd, nblk, width, prefix)),
         out_shape=jax.ShapeDtypeStruct((nblk, BLK, width), BF16),
-        in_specs=[smem, smem, vmem, vmem, vmem, vmem, vmem, hbm, hbm, hbm, hbm, hbm],
-        out_specs=vmem,
+        in_specs=[hbm] * 12,
+        out_specs=pl.BlockSpec(memory_space=pltpu.VMEM),
         scratch_shapes=[
+            pltpu.SMEM((1,), jnp.int32),
+            pltpu.SMEM((1,), jnp.int32),
+            pltpu.VMEM((1, nblk), jnp.int32),
+            pltpu.VMEM((1, nblk), jnp.int32),
+            pltpu.VMEM((1, width), F32),
+            pltpu.VMEM((1, 4 * width), F32),
+            pltpu.VMEM((1, width), F32),
+            block,
             pltpu.VMEM((nblk, BLK, width), BF16),
             pltpu.VMEM((prefix, width), BF16),
             pltpu.VMEM((width, prefix), BF16),
             pltpu.VMEM((prefix, width), BF16),
             pltpu.VMEM((width, 4 * width), BF16),
             pltpu.VMEM((width, width), BF16),
-            pltpu.VMEM((tile_rows, 4 * width), BF16),
-            pltpu.VMEM((nblk, BLK // CHUNKS, width), BF16),
+            pltpu.VMEM((tile_rows, width), BF16),
+            pltpu.VMEM((tile_rows, width), BF16),
+            pltpu.VMEM((tile_rows, 3 * width), BF16),
+            pltpu.VMEM((tile_rows, width), F32),
             table,
             pltpu.VMEM((ng, 8, 128), jnp.int32),
             pltpu.VMEM((nd, 8, 128), jnp.int32),
@@ -515,14 +601,14 @@
             pltpu.VMEM((ng, 8, 128), jnp.int32),
             table,
             pltpu.SMEM((8, 128), jnp.int32),
-            pltpu.SemaphoreType.DMA((5,)),
+            pltpu.SemaphoreType.DMA((13,)),
             pltpu.SemaphoreType.DMA,
             pltpu.SemaphoreType.DMA((4,)),
             pltpu.SemaphoreType.DMA((4,)),
-            pltpu.SemaphoreType.DMA((4, CHUNKS)),
-            pltpu.SemaphoreType.DMA((4, CHUNKS)),
+            pltpu.SemaphoreType.DMA((2, CHUNKS)),
+            pltpu.SemaphoreType.DMA((2, CHUNKS)),
         ]
-        + [block] * (8 * CHUNKS),
+        + [block] * (4 * CHUNKS),
         compiler_params=pltpu.CompilerParams(
             collective_id=0, has_side_effects=True, vmem_limit_bytes=60 * 2**20
         ),

time: 58.8 us -> 48.9 us (0.83)
  Pallas kernels: 53.8 us -> 44.4 us
    pallas_call x1, Pallas kernels: 53.8 us -> 44.4 us  [layer(): pl.pallas_call(functools.partial(kernel, (ng, nd, nblk, width, prefix)),...]
where the time goes in v2:
time: 48.9 us; the launch traced here: 48.8 us
  Pallas kernels  44.4 us (91%)
  local copies, waits for them, and re-layouts  3.05 us (6%)
  between operations  1.3 us (3%)
    pallas_call x1, Pallas kernels, layer(): pl.pallas_call(functools.partial(kernel, (ng, nd, nblk, width, prefix)),...  44.4 us
    unnamed x1, local copies, waits for them, and re-layouts  3.05 us

profile of v2, /device:TPU:1, one launch (start us, length us, event | category | flops | bytes accessed | tf_op | source)
XLA Modules:
  0.0 48.8 jit_solution(3962472655753655168)
XLA Ops:
  1.3 44.4 %shard_map.118 = bf16[16,128,512]{2,1,0:T(8,128)(2,1)} custom-call(s32[1]{0:T(128)S(6)} %copy.14.refs_0_, s32[1]{0:T(128)S(6)} %copy.15.refs_1_, s32[1,16]{1,0:T(1,128)} %bitcast.16, s32[1,16]{1,0:T(1,128)} %bitcast.17, f32[1,512]{1,0:T(1,128)} %bitcast.14, f32[1,2048]{1,0:T(1,128)} %bitcast.13, f32[1,512]{1,0:T(1,128)} %bitcast.15, ...), custom_call_target="tpu_custom_call" | custom-call | tf_op jit(solution)/shard_map/pallas_call | solution.py:571
  45.7 3.0 %copy.16 = bf16[2048,512]{1,0:T(8,128)(2,1)} copy(bf16[2048,512]{1,0:T(8,128)(2,1)} %bitcast.9) | data formatting | bytes 4194304

commit v3 on v2

--- a/solution.py
+++ b/solution.py
@@ -12,13 +12,18 @@
 CHUNKS = 8
 LAG = 4
 LAST_LAG = 7
+HALVED = (6, 7)
 KEY_TILE = 256
 AHEAD = 2
 COLS = 256
 MESH = pl.DeviceIdType.MESH
 F32 = jnp.float32
 BF16 = jnp.bfloat16
-ORDER_G, ORDER_D, PICK_1, PICK_2, SLOT_1, SLOT_2 = range(6)
+ORDER_G, ORDER_D, PICK_1, PICK_2, SLOT_1, SLOT_2, MOVE = range(7)
+
+
+def in_hbm(array):
+    return pltpu.with_memory_space_constraint(array, pltpu.HBM)
 
 
 def log2(number):
@@ -52,6 +57,16 @@
     centred = matrix - average
     spread = jnp.sum(centred * centred, axis=-1, keepdims=True) * (1.0 / width)
     return centred * lax.rsqrt(spread + 1e-06)
+
+
+def routes_of(width):
+    routes = []
+    for c in range(CHUNKS):
+        if c in HALVED:
+            routes += [(c, way, way * (width // 2), width // 2) for way in (0, 1)]
+        else:
+            routes.append((c, c % 2, 0, width))
+    return routes
 
 
 def half_silu(half):
@@ -91,6 +106,7 @@
         values,
         win,
         wout,
+        whole,
         nrm,
         gate,
         qkv,
@@ -112,7 +128,10 @@
         data_recv,
         *bufs,
     ) = refs
-    send_a, recv_a, send_b, recv_b = (bufs[CHUNKS * k : CHUNKS * (k + 1)] for k in range(4))
+    routes = routes_of(width)
+    send_a, recv_a, send_b, recv_b = (
+        bufs[len(routes) * k : len(routes) * (k + 1)] for k in range(4)
+    )
     me_g = lax.axis_index("grp")
     me_d = lax.axis_index("dev")
 
@@ -195,9 +214,14 @@
             high = jnp.where(hit_g, jnp.maximum(high, i), high)
             order_d = jnp.where(column(member, i) == want_d, i, order_d)
         order_g = jnp.where((lane & 1) == 0, low, high)
+        move = jnp.zeros((8, 128), jnp.int32)
+        for place in range(nblk):
+            move = jnp.where(column(order_g, place) == order_d, place, move)
         row = rows_of((8, 128))
         idx_v[...] = jnp.where(
-            row == ORDER_G, order_g, jnp.where(row == ORDER_D, order_d, 0)
+            row == ORDER_G,
+            order_g,
+            jnp.where(row == ORDER_D, order_d, jnp.where(row == MOVE, move, 0)),
         )
         tab_g[0] = table
         tab_d[0] = table
@@ -322,22 +346,22 @@
     def look(row, lane):
         return idx[row, lane] & (nblk - 1)
 
-    def remote(src, dst, stage, c, where):
+    def remote(src, dst, stage, r, where):
         return pltpu.make_async_remote_copy(
-            src, dst, data_send.at[stage, c], data_recv.at[stage, c], where, MESH
+            src, dst, data_send.at[stage, r], data_recv.at[stage, r], where, MESH
         )
 
-    def to_groups(src, dst, stage, c):
+    def to_groups(src, dst, stage, r):
         def step(number, carry):
             span = pl.ds(2 * number, 2)
-            remote(src.at[span], dst.at[span], stage, c, at_group(number)).start()
+            remote(src.at[span], dst.at[span], stage, r, at_group(number)).start()
             return carry
 
         lax.fori_loop(1, ng, step, 0)
 
-    def to_members(src, dst, stage, c):
+    def to_members(src, dst, stage, r):
         def step(number, carry):
-            remote(src.at[number], dst.at[number], stage, c, at_member(number)).start()
+            remote(src.at[number], dst.at[number], stage, r, at_member(number)).start()
             return carry
 
         lax.fori_loop(1, nd, step, 0)
@@ -345,36 +369,44 @@
     def far(ref, by_group):
         return ref.at[pl.ds(2, nblk - 2)] if by_group else ref.at[pl.ds(1, nd - 1)]
 
-    def send_first(c):
-        (to_groups if c % 2 else to_members)(send_a[c], recv_a[c], 0, c)
-
-    def send_second(c):
-        wait_bytes(data_recv.at[0, c], far(recv_a[c], c % 2))
-        near = 1 if c % 2 else 2
-        pick = PICK_1 if c % 2 else PICK_2
+    def send_first(r):
+        way = routes[r][1]
+        (to_groups if way else to_members)(send_a[r], recv_a[r], 0, r)
+
+    def send_second(r):
+        way = routes[r][1]
+        wait_bytes(data_recv.at[0, r], far(recv_a[r], way))
+        near = 1 if way else 2
+        pick = PICK_1 if way else PICK_2
         for k in range(near):
-            recv_b[c][k] = recv_a[c][look(pick, k)]
+            recv_b[r][k] = recv_a[r][look(pick, k)]
 
         def step(number, carry):
             for k in range(near):
-                send_b[c][near * number + k] = recv_a[c][look(pick, near * number + k)]
+                send_b[r][near * number + k] = recv_a[r][look(pick, near * number + k)]
             span = pl.ds(near * number, near)
-            where = at_member(number) if c % 2 else at_group(number)
-            remote(send_b[c].at[span], recv_b[c].at[span], 1, c, where).start()
+            where = at_member(number) if way else at_group(number)
+            remote(send_b[r].at[span], recv_b[r].at[span], 1, r, where).start()
             return carry
 
         lax.fori_loop(1, nblk // near, step, 0)
 
-    def deliver(c):
-        wait_bytes(data_recv.at[1, c], far(recv_b[c], c % 2 == 0))
+    def deliver(r):
+        c, way, first, wide = routes[r]
+        wait_bytes(data_recv.at[1, r], far(recv_b[r], not way))
 
         def step(number, carry):
             for s in (2 * number, 2 * number + 1):
-                slot = look(SLOT_1 if c % 2 else SLOT_2, s)
-                out_ref[s, c * piece : (c + 1) * piece, :] = recv_b[c][slot]
+                slot = look(SLOT_1 if way else SLOT_2, s)
+                out_ref[s, c * piece : (c + 1) * piece, first : first + wide] = recv_b[r][slot]
             return carry
 
         lax.fori_loop(0, nblk // 2, step, 0)
+
+    def each_route(action, c):
+        for r, route in enumerate(routes):
+            if route[0] == c:
+                action(r)
 
     def prepare_prefix():
         load_keys.wait()
@@ -394,7 +426,10 @@
     score_scale = 0.5 / (head_dim**0.5)
 
     def order_of(t):
-        return jnp.where(t % 2 == 1, ORDER_G, ORDER_D)
+        by_group = t % 2 == 1
+        for c in HALVED:
+            by_group = jnp.logical_or(by_group, t == c)
+        return jnp.where(by_group, ORDER_G, ORDER_D)
 
     def rows_in_order(ref, t, first_row):
         row = order_of(t)
@@ -404,7 +439,10 @@
         return jnp.concatenate(parts, axis=0).astype(F32)
 
     def normalise_rows(ref, t, first_row):
-        x = rows_in_order(ref, t, first_row)
+        if ref is cand_first:
+            x = cand_first[...].reshape(tile_rows, width).astype(F32)
+        else:
+            x = rows_in_order(ref, t, first_row)
         nrm[...] = (centre(x, width) * (gain_ref[...] * 0.5)).astype(BF16)
 
     def project(first):
@@ -460,49 +498,67 @@
             centre(att[...], width) * again_ref[...] * gate[...].astype(F32)
         ).astype(BF16)
 
-    def finish(t, gated):
-        first_row = pl.multiple_of(t * piece, piece)
+    def finish(t, gated, stored_order=False):
+        first_row = t * piece if stored_order else pl.multiple_of(t * piece, piece)
         delta = jnp.dot(gated, wout[...], preferred_element_type=F32)
         row = order_of(t)
         count = count_ref[0]
         done = []
         for place in range(nblk):
-            block = look(row, place)
+            block = place if stored_order else look(row, place)
             x = cand[block, pl.ds(first_row, piece), :].astype(F32)
             x = x + delta[place * piece : (place + 1) * piece, :]
             live = rows_of((piece, width)) + (block * BLK + first_row) < count
             done.append(jnp.where(live, x, 0.0).astype(BF16))
         return done
 
+    def store(c, done):
+        if c in HALVED:
+            for place in range(nblk):
+                whole[place] = done[place]
+
+        def keep(r):
+            way, first, wide = routes[r][1:]
+            near = 2 if way else 1
+            for place in range(nblk):
+                target = recv_a[r] if place < near else send_a[r]
+                if c in HALVED and not way:
+                    target[place] = whole[look(MOVE, place), :, first : first + wide]
+                else:
+                    target[place] = done[place][:, first : first + wide]
+            send_first(r)
+
+        each_route(keep, c)
+
+    def serve(c):
+        if c == LAG:
+            middle_tables()
+        if 0 <= c - LAG < CHUNKS:
+            each_route(send_second, c - LAG)
+        if c == LAST_LAG:
+            final_tables()
+        if 0 <= c - LAST_LAG < CHUNKS:
+            each_route(deliver, c - LAST_LAG)
+
     def exchange(t, done):
-        for c in range(CHUNKS):
+        for c in range(1, CHUNKS):
 
             @pl.when(t == c)
             def _():
-                near = 2 if c % 2 else 1
-                for place in range(nblk):
-                    (recv_a[c] if place < near else send_a[c])[place] = done[place]
-                send_first(c)
-                if c == LAG:
-                    middle_tables()
-                if c >= LAG:
-                    send_second(c - LAG)
-                if c == LAST_LAG:
-                    final_tables()
-                if c >= LAST_LAG:
-                    deliver(c - LAST_LAG)
-
+                store(c, done)
+                serve(c)
+
+    load_first.wait()
+    load_gain.wait()
+    normalise_rows(cand_first, 0, 0)
     load_device.wait()
     load_slot.wait()
     own_table()
-    publish()
-    load_first.wait()
-    load_gain.wait()
-    normalise_rows(cand_first, 0, 0)
     load_bias.wait()
     load_win.wait()
     project_qkv()
     prepare_prefix()
+    publish()
     load_cand.wait()
 
     def next_rows(t):
@@ -512,8 +568,15 @@
     load_again.wait()
     load_count.wait()
     load_wout.wait()
+    done = finish(0, finish_gate(), True)
+    for place in range(nblk):
+        whole[place] = done[place]
+    done = [whole[look(ORDER_D, place)] for place in range(nblk)]
     pl.semaphore_wait(barrier, ng + nd - 2)
+    store(0, done)
     send_tables()
+    project_qkv()
+    attend(lambda: next_rows(2))
 
     def step(t, carry):
         gated = finish_gate()
@@ -523,25 +586,26 @@
         attend(lambda: next_rows(jnp.minimum(t + 1, CHUNKS - 1)))
         return carry
 
-    lax.fori_loop(1, CHUNKS, step, 0)
+    lax.fori_loop(2, CHUNKS, step, 0)
     last = CHUNKS - 1
-    exchange(last, finish(last, finish_gate()))
+    store(last, finish(last, finish_gate()))
+    serve(last)
     waiting = CHUNKS - LAST_LAG
     for c in range(CHUNKS - LAG, CHUNKS):
-        send_second(c)
+        each_route(send_second, c)
         if waiting < c - 1:
-            deliver(waiting)
+            each_route(deliver, waiting)
             waiting += 1
     for c in range(waiting, CHUNKS):
-        deliver(c)
+        each_route(deliver, c)
 
     wait_bytes(meta_send.at[0], tab_g.at[pl.ds(1, ng - 1)])
     wait_bytes(meta_send.at[1], tab_d.at[pl.ds(1, nd - 1)])
     wait_bytes(meta_send.at[2], slot_in_1.at[pl.ds(1, nd - 1)])
     wait_bytes(meta_send.at[3], slot_in_2.at[pl.ds(1, ng - 1)])
-    for c in range(CHUNKS):
-        wait_bytes(data_send.at[0, c], far(send_a[c], c % 2))
-        wait_bytes(data_send.at[1, c], far(send_b[c], c % 2 == 0))
+    for r, route in enumerate(routes):
+        wait_bytes(data_send.at[0, r], far(send_a[r], route[1]))
+        wait_bytes(data_send.at[1, r], far(send_b[r], not route[1]))
 
 
 def layer(
@@ -566,6 +630,7 @@
     piece = BLK // CHUNKS
     tile_rows = nblk * piece
     hbm = pl.BlockSpec(memory_space=pl.ANY)
+    routes = routes_of(width)
     block = pltpu.VMEM((nblk, piece, width), BF16)
     table = pltpu.VMEM((8, 128), jnp.int32)
     out = pl.pallas_call(
@@ -588,6 +653,7 @@
             pltpu.VMEM((prefix, width), BF16),
             pltpu.VMEM((width, 4 * width), BF16),
             pltpu.VMEM((width, width), BF16),
+            block,
             pltpu.VMEM((tile_rows, width), BF16),
             pltpu.VMEM((tile_rows, width), BF16),
             pltpu.VMEM((tile_rows, 3 * width), BF16),
@@ -605,26 +671,31 @@
             pltpu.SemaphoreType.DMA,
             pltpu.SemaphoreType.DMA((4,)),
             pltpu.SemaphoreType.DMA((4,)),
-            pltpu.SemaphoreType.DMA((2, CHUNKS)),
-            pltpu.SemaphoreType.DMA((2, CHUNKS)),
+            pltpu.SemaphoreType.DMA((2, len(routes))),
+            pltpu.SemaphoreType.DMA((2, len(routes))),
         ]
-        + [block] * (4 * CHUNKS),
+        + [pltpu.VMEM((nblk, piece, route[3]), BF16) for route in routes] * 4,
         compiler_params=pltpu.CompilerParams(
-            collective_id=0, has_side_effects=True, vmem_limit_bytes=60 * 2**20
+            collective_id=0, has_side_effects=True, vmem_limit_bytes=40 * 2**20
         ),
     )(
         cand_count,
         prefix_len,
-        dest_device.reshape(1, nblk),
-        dest_slot.reshape(1, nblk),
-        norm_gain.reshape(1, width),
-        b_in.reshape(1, 4 * width),
-        attn_gain.reshape(1, width),
-        candidates.reshape(nblk, BLK, width),
-        prefix_keys[0],
-        prefix_values[0],
-        w_in,
-        w_out,
+        *map(
+            in_hbm,
+            (
+                dest_device.reshape(1, nblk),
+                dest_slot.reshape(1, nblk),
+                norm_gain.reshape(1, width),
+                b_in.reshape(1, 4 * width),
+                attn_gain.reshape(1, width),
+                candidates.reshape(nblk, BLK, width),
+                prefix_keys[0],
+                prefix_values[0],
+                w_in,
+                w_out,
+            ),
+        )
     )
     return out.reshape(rows, width)
 

time: 48.9 us -> 46.1 us (0.943)
  local copies, waits for them, and re-layouts: 3.05 us -> 1.32 us
  Pallas kernels: 44.4 us -> 43.4 us
    unnamed x1, local copies, waits for them, and re-layouts: 3.05 us -> 1.32 us
    pallas_call x1, Pallas kernels: 44.4 us -> 43.4 us  [layer(): pl.pallas_call(functools.partial(kernel, (ng, nd, nblk, width, prefix)),...]
where the time goes in v3:
time: 46.1 us; the launch traced here: 46 us
  Pallas kernels  43.4 us (94%)
  local copies, waits for them, and re-layouts  1.32 us (3%)
  between operations  1.3 us (3%)
    pallas_call x1, Pallas kernels, layer(): pl.pallas_call(functools.partial(kernel, (ng, nd, nblk, width, prefix)),...  43.4 us
    unnamed x1, local copies, waits for them, and re-layouts  1.32 us

profile of v3, /device:TPU:1, one launch (start us, length us, event | category | flops | bytes accessed | tf_op | source)
XLA Modules:
  0.0 46.0 jit_solution(631204909730361656)
XLA Ops:
  1.3 43.4 %shard_map.118 = bf16[16,128,512]{2,1,0:T(8,128)(2,1)S(1)} custom-call(s32[1]{0:T(128)S(6)} %copy.14.refs_0_, s32[1]{0:T(128)S(6)} %copy.15.refs_1_, s32[1,16]{1,0:T(1,128)} %bitcast.16, s32[1,16]{1,0:T(1,128)} %bitcast.17, f32[1,512]{1,0:T(1,128)} %bitcast.14, f32[1,2048]{1,0:T(1,128)} %bitcast.13, f32[1,512]{1,0:T(1,128)} %bitcast.15, ...), custom_call_target="tpu_custom_call" | custom-call | tf_op jit(solution)/shard_map/pallas_call | solution.py:636
  44.7 1.3 %copy.16 = bf16[2048,512]{1,0:T(8,128)(2,1)} copy(bf16[2048,512]{1,0:T(8,128)(2,1)S(1)} %bitcast.9) | data formatting | bytes 4194304

commit v4 on v3

--- a/solution.py
+++ b/solution.py
@@ -11,8 +11,8 @@
 BLK = 128
 CHUNKS = 8
 LAG = 4
-LAST_LAG = 7
-HALVED = (6, 7)
+LAST_LAG = 8
+HALVED = (1, 2, 3, 4, 5, 6, 7)
 KEY_TILE = 256
 AHEAD = 2
 COLS = 256
@@ -357,14 +357,14 @@
             remote(src.at[span], dst.at[span], stage, r, at_group(number)).start()
             return carry
 
-        lax.fori_loop(1, ng, step, 0)
+        lax.fori_loop(1, ng, step, 0, unroll=True)
 
     def to_members(src, dst, stage, r):
         def step(number, carry):
             remote(src.at[number], dst.at[number], stage, r, at_member(number)).start()
             return carry
 
-        lax.fori_loop(1, nd, step, 0)
+        lax.fori_loop(1, nd, step, 0, unroll=True)
 
     def far(ref, by_group):
         return ref.at[pl.ds(2, nblk - 2)] if by_group else ref.at[pl.ds(1, nd - 1)]
@@ -378,30 +378,25 @@
         wait_bytes(data_recv.at[0, r], far(recv_a[r], way))
         near = 1 if way else 2
         pick = PICK_1 if way else PICK_2
-        for k in range(near):
-            recv_b[r][k] = recv_a[r][look(pick, k)]
+        for place in range(nblk):
+            target = recv_b[r] if place < near else send_b[r]
+            target[place] = recv_a[r][look(pick, place)]
 
         def step(number, carry):
-            for k in range(near):
-                send_b[r][near * number + k] = recv_a[r][look(pick, near * number + k)]
             span = pl.ds(near * number, near)
             where = at_member(number) if way else at_group(number)
             remote(send_b[r].at[span], recv_b[r].at[span], 1, r, where).start()
             return carry
 
-        lax.fori_loop(1, nblk // near, step, 0)
+        lax.fori_loop(1, nblk // near, step, 0, unroll=True)
 
     def deliver(r):
         c, way, first, wide = routes[r]
         wait_bytes(data_recv.at[1, r], far(recv_b[r], not way))
 
-        def step(number, carry):
-            for s in (2 * number, 2 * number + 1):
-                slot = look(SLOT_1 if way else SLOT_2, s)
-                out_ref[s, c * piece : (c + 1) * piece, first : first + wide] = recv_b[r][slot]
-            return carry
-
-        lax.fori_loop(0, nblk // 2, step, 0)
+        for s in range(nblk):
+            slot = look(SLOT_1 if way else SLOT_2, s)
+            out_ref[s, c * piece : (c + 1) * piece, first : first + wide] = recv_b[r][slot]
 
     def each_route(action, c):
         for r, route in enumerate(routes):
@@ -590,10 +585,12 @@
     last = CHUNKS - 1
     store(last, finish(last, finish_gate()))
     serve(last)
-    waiting = CHUNKS - LAST_LAG
+    if LAST_LAG >= CHUNKS:
+        final_tables()
+    waiting = max(CHUNKS - LAST_LAG, 0)
     for c in range(CHUNKS - LAG, CHUNKS):
         each_route(send_second, c)
-        if waiting < c - 1:
+        if waiting < c - 2:
             each_route(deliver, waiting)
             waiting += 1
     for c in range(waiting, CHUNKS):

time: 46.1 us -> 44.8 us (0.972)
  Pallas kernels: 43.4 us -> 42 us
    pallas_call x1, Pallas kernels: 43.4 us -> 42 us  [layer(): pl.pallas_call(functools.partial(kernel, (ng, nd, nblk, width, prefix)),...]
where the time goes in v4:
time: 44.8 us; the launch traced here: 44.7 us
  Pallas kernels  42 us (94%)
  local copies, waits for them, and re-layouts  1.32 us (3%)
  between operations  1.3 us (3%)
    pallas_call x1, Pallas kernels, layer(): pl.pallas_call(functools.partial(kernel, (ng, nd, nblk, width, prefix)),...  42 us
    unnamed x1, local copies, waits for them, and re-layouts  1.32 us

profile of v4, /device:TPU:1, one launch (start us, length us, event | category | flops | bytes accessed | tf_op | source)
XLA Modules:
  0.0 44.7 jit_solution(7683465196443023981)
XLA Ops:
  1.3 42.0 %shard_map.118 = bf16[16,128,512]{2,1,0:T(8,128)(2,1)S(1)} custom-call(s32[1]{0:T(128)S(6)} %copy.14.refs_0_, s32[1]{0:T(128)S(6)} %copy.15.refs_1_, s32[1,16]{1,0:T(1,128)} %bitcast.16, s32[1,16]{1,0:T(1,128)} %bitcast.17, f32[1,512]{1,0:T(1,128)} %bitcast.14, f32[1,2048]{1,0:T(1,128)} %bitcast.13, f32[1,512]{1,0:T(1,128)} %bitcast.15, ...), custom_call_target="tpu_custom_call" | custom-call | tf_op jit(solution)/shard_map/pallas_call | solution.py:633
  43.4 1.3 %copy.16 = bf16[2048,512]{1,0:T(8,128)(2,1)} copy(bf16[2048,512]{1,0:T(8,128)(2,1)S(1)} %bitcast.9) | data formatting | bytes 4194304

commit v5 on v4

--- a/solution.py
+++ b/solution.py
@@ -10,9 +10,8 @@
 HEADS = 4
 BLK = 128
 CHUNKS = 8
-LAG = 4
-LAST_LAG = 8
-HALVED = (1, 2, 3, 4, 5, 6, 7)
+SECOND = {4: 0, 5: 1, 6: 2, 7: 3}
+HALVED = (7,)
 KEY_TILE = 256
 AHEAD = 2
 COLS = 256
@@ -526,14 +525,10 @@
         each_route(keep, c)
 
     def serve(c):
-        if c == LAG:
+        if c == min(SECOND):
             middle_tables()
-        if 0 <= c - LAG < CHUNKS:
-            each_route(send_second, c - LAG)
-        if c == LAST_LAG:
-            final_tables()
-        if 0 <= c - LAST_LAG < CHUNKS:
-            each_route(deliver, c - LAST_LAG)
+        if c in SECOND:
+            each_route(send_second, SECOND[c])
 
     def exchange(t, done):
         for c in range(1, CHUNKS):
@@ -585,15 +580,11 @@
     last = CHUNKS - 1
     store(last, finish(last, finish_gate()))
     serve(last)
-    if LAST_LAG >= CHUNKS:
-        final_tables()
-    waiting = max(CHUNKS - LAST_LAG, 0)
-    for c in range(CHUNKS - LAG, CHUNKS):
+    for c in range(len(SECOND), last):
         each_route(send_second, c)
-        if waiting < c - 2:
-            each_route(deliver, waiting)
-            waiting += 1
-    for c in range(waiting, CHUNKS):
+    each_route(send_second, last)
+    final_tables()
+    for c in range(CHUNKS):
         each_route(deliver, c)
 
     wait_bytes(meta_send.at[0], tab_g.at[pl.ds(1, ng - 1)])

time: 44.8 us -> 44 us (0.982)
  Pallas kernels: 42 us -> 41.3 us
    pallas_call x1, Pallas kernels: 42 us -> 41.3 us  [layer(): pl.pallas_call(functools.partial(kernel, (ng, nd, nblk, width, prefix)),...]
where the time goes in v5:
time: 44 us; the launch traced here: 43.9 us
  Pallas kernels  41.3 us (94%)
  local copies, waits for them, and re-layouts  1.32 us (3%)
  between operations  1.3 us (3%)
    pallas_call x1, Pallas kernels, layer(): pl.pallas_call(functools.partial(kernel, (ng, nd, nblk, width, prefix)),...  41.3 us
    unnamed x1, local copies, waits for them, and re-layouts  1.32 us

profile of v5, /device:TPU:1, one launch (start us, length us, event | category | flops | bytes accessed | tf_op | source)
XLA Modules:
  0.0 43.9 jit_solution(602111757177170912)
XLA Ops:
  1.3 41.3 %shard_map.118 = bf16[16,128,512]{2,1,0:T(8,128)(2,1)S(1)} custom-call(s32[1]{0:T(128)S(6)} %copy.14.refs_0_, s32[1]{0:T(128)S(6)} %copy.15.refs_1_, s32[1,16]{1,0:T(1,128)} %bitcast.16, s32[1,16]{1,0:T(1,128)} %bitcast.17, f32[1,512]{1,0:T(1,128)} %bitcast.14, f32[1,2048]{1,0:T(1,128)} %bitcast.13, f32[1,512]{1,0:T(1,128)} %bitcast.15, ...), custom_call_target="tpu_custom_call" | custom-call | tf_op jit(solution)/shard_map/pallas_call | solution.py:624
  42.6 1.3 %copy.16 = bf16[2048,512]{1,0:T(8,128)(2,1)} copy(bf16[2048,512]{1,0:T(8,128)(2,1)S(1)} %bitcast.9) | data formatting | bytes 4194304

commit v6 on v5

--- a/solution.py
+++ b/solution.py
@@ -119,6 +119,7 @@
         slot_in_2,
         idx_v,
         idx,
+        idx_mid,
         load_sem,
         idx_sem,
         meta_send,
@@ -317,7 +318,7 @@
 
         lax.fori_loop(1, nd, to_member, 0)
         lax.fori_loop(1, ng, to_group, 0)
-        publish()
+        pltpu.make_async_copy(idx_v, idx_mid, idx_sem).start()
 
     def final_tables():
         wait_bytes(meta_recv.at[2], slot_in_1.at[pl.ds(1, nd - 1)])
@@ -343,7 +344,9 @@
         publish()
 
     def look(row, lane):
-        return idx[row, lane] & (nblk - 1)
+        middle = isinstance(row, int) and row in (PICK_1, PICK_2)
+        table = idx_mid if middle else idx
+        return table[row, lane] & (nblk - 1)
 
     def remote(src, dst, stage, r, where):
         return pltpu.make_async_remote_copy(
@@ -525,8 +528,10 @@
         each_route(keep, c)
 
     def serve(c):
+        if c == min(SECOND) - 1:
+            middle_tables()
         if c == min(SECOND):
-            middle_tables()
+            pltpu.make_async_copy(idx_v, idx_mid, idx_sem).wait()
         if c in SECOND:
             each_route(send_second, SECOND[c])
 
@@ -655,6 +660,7 @@
             pltpu.VMEM((ng, 8, 128), jnp.int32),
             table,
             pltpu.SMEM((8, 128), jnp.int32),
+            pltpu.SMEM((8, 128), jnp.int32),
             pltpu.SemaphoreType.DMA((13,)),
             pltpu.SemaphoreType.DMA,
             pltpu.SemaphoreType.DMA((4,)),

time: 44 us -> 43.9 us (level)
  no operation moved by 1% of the time
where the time goes in v6:
time: 43.9 us; the launch traced here: 43.8 us
  Pallas kernels  41.2 us (94%)
  local copies, waits for them, and re-layouts  1.32 us (3%)
  between operations  1.3 us (3%)
    pallas_call x1, Pallas kernels, layer(): pl.pallas_call(functools.partial(kernel, (ng, nd, nblk, width, prefix)),...  41.2 us
    unnamed x1, local copies, waits for them, and re-layouts  1.32 us

profile of v6, /device:TPU:1, one launch (start us, length us, event | category | flops | bytes accessed | tf_op | source)
XLA Modules:
  0.0 43.8 jit_solution(9350640363052400116)
XLA Ops:
  1.3 41.2 %shard_map.118 = bf16[16,128,512]{2,1,0:T(8,128)(2,1)S(1)} custom-call(s32[1]{0:T(128)S(6)} %copy.14.refs_0_, s32[1]{0:T(128)S(6)} %copy.15.refs_1_, s32[1,16]{1,0:T(1,128)} %bitcast.16, s32[1,16]{1,0:T(1,128)} %bitcast.17, f32[1,512]{1,0:T(1,128)} %bitcast.14, f32[1,2048]{1,0:T(1,128)} %bitcast.13, f32[1,512]{1,0:T(1,128)} %bitcast.15, ...), custom_call_target="tpu_custom_call" | custom-call | tf_op jit(solution)/shard_map/pallas_call | solution.py:629
  42.5 1.3 %copy.16 = bf16[2048,512]{1,0:T(8,128)(2,1)} copy(bf16[2048,512]{1,0:T(8,128)(2,1)S(1)} %bitcast.9) | data formatting | bytes 4194304
